TPU v7x, 256 devices: a whole 4x4x8 slice. The times are simulated.
256 devices in a mesh: row: 16 (over y, x), col: 16 (over z, core).
Axes of the slice: x: 4, y: 4, z: 8, core: 2. Of those that a mesh axis runs over, the one named last changes fastest.
Arguments:
- coeffs: bfloat16 [16384, 2048], P('row'), may hold values from -1 to 1
- p_slots: int32 [16, 16, 8], P('row', 'col'), may hold values from 0 to 63, as said below
- p_count: int32 [16, 16], P('row', 'col'), may hold values from 1 to 8
- s_blocks: bfloat16 [16, 16, 8, 128, 128], P('row', 'col'), may hold values from -0.3984375 to 0.3984375
- s_slots: int32 [16, 16, 8], P('row', 'col'), may hold values from 0 to 63, as said below
- s_count: int32 [16, 16], P('row', 'col'), may hold values from 1 to 8
- q_slots: int32 [16, 16, 8], P('row', 'col'), may hold values from 0 to 63, as said below
- q_count: int32 [16, 16], P('row', 'col'), may hold values from 1 to 8
Outputs:
- density: bfloat16 [16, 16, 8, 128, 128], P('row', 'col')
- product: float32 [16, 16, 8, 128, 128], P('row', 'col')
Inputs may be any that keep to these rules, and one draw needn't show every extreme that they name: `p_slots`: on each device the live slots name different blocks of its tile; at least one device has all 8 slots live, which one is drawn. `s_slots`: on each device the live slots name different positions; at least one device has all 8 slots live, which one is drawn. `q_slots`: on each device the live slots name different blocks of its tile; at least one device has all 8 slots live, which one is drawn.
All inputs are finite; a program needn't handle non-finite values.
Results may differ from a plain program's by a relative error of at most 0.0029.
Values may be sent and summed in bfloat16 or wider, within the bound.
A program may use at most 192 MiB of HBM per device.

v0:
```python
import jax
import jax.numpy as jnp
from jax import lax
from jax.sharding import PartitionSpec as P


def from_root(block, axis, source):
    block = jnp.where(lax.axis_index(axis) == source, block, jnp.zeros_like(block))
    return lax.psum(block, axis)


def shortened(shard):

    def short(part):
        return part.astype(jnp.bfloat16) if part.dtype == jnp.float32 else part

    return jax.tree.map(short, shard)


def shifted(block, axis, distance):
    devices = range(lax.axis_size(axis))
    route = [((i - distance) % len(devices), i) for i in devices]
    return lax.ppermute(block, axis, route)


def step_product(summed, p_data, s_data, panel_slot, q_row, q_col, tile_cols):
    p_blocks, p_code = p_data
    s_blocks, s_code = s_data
    local_k = jnp.arange(tile_cols, dtype=jnp.int32)
    p_live = p_code >= 0
    p_row = jnp.where(p_live, p_code // tile_cols, -1)
    p_col = jnp.where(p_live, p_code % tile_cols, -1)
    pick_left = (
        (p_row[:, None, None] == q_row[None, :, None])
        & (p_col[:, None, None] == local_k[None, None, :])
    ).astype(jnp.bfloat16)
    left_rows = jnp.einsum("pqk,pab->qakb", pick_left, p_blocks, preferred_element_type=jnp.float32)
    left_rows = left_rows.astype(jnp.bfloat16).reshape(q_row.shape[0], 128, tile_cols * 128)
    square = tile_cols * tile_cols
    s_live = (s_code >= 0) & (s_code // square == panel_slot)
    s_local = s_code % square
    s_row = jnp.where(s_live, s_local // tile_cols, -1)
    s_col = s_local % tile_cols
    pick_right = (
        (s_row[:, None, None] == local_k[None, :, None])
        & (s_col[:, None, None] == q_col[None, None, :])
    ).astype(jnp.bfloat16)
    right_cols = jnp.einsum(
        "skq,sab->kaqb", pick_right, s_blocks, preferred_element_type=jnp.float32
    )
    right_cols = right_cols.astype(jnp.bfloat16).reshape(tile_cols * 128, q_row.shape[0], 128)
    return summed + jnp.einsum(
        "qak,kqb->qab", left_rows, right_cols, preferred_element_type=jnp.float32
    )


def pick_tree(flag, moved, kept):
    return jax.tree.map(lambda fresh, stale: jnp.where(flag, fresh, stale), moved, kept)


def on_device(coeffs, p_slots, p_count, s_blocks, s_slots, s_count, q_slots, q_count):
    rows_n = lax.axis_size("row")
    cols_n = lax.axis_size("col")
    row_at = lax.axis_index("row")
    col_at = lax.axis_index("col")
    panel_rows, orbitals = coeffs.shape
    tile_rows = panel_rows // 128
    tile_cols = panel_rows * rows_n // cols_n // 128
    sub_span = cols_n // rows_n
    source = from_root(coeffs, "row", col_at // sub_span)
    slot_ids = p_slots[0, 0]
    p_max = slot_ids.shape[0]
    p_live = jnp.arange(p_max, dtype=jnp.int32) < p_count[0, 0]
    left = coeffs.reshape(tile_rows, 128, orbitals)[slot_ids // tile_cols]
    right = source.reshape(tile_cols, 128, orbitals)[slot_ids % tile_cols]
    raw = jnp.einsum("pak,pbk->pab", left, right, preferred_element_type=jnp.float32)
    dense_blocks = jnp.where(p_live[:, None, None], raw, jnp.zeros_like(raw)).astype(jnp.bfloat16)
    p_code = jnp.where(p_live, slot_ids, -1)
    s_ids = s_slots[0, 0]
    s_max = s_ids.shape[0]
    s_live = jnp.arange(s_max, dtype=jnp.int32) < s_count[0, 0]
    s_code = jnp.where(s_live, s_ids, -1)
    s_local = s_blocks[0, 0]
    q_ids = q_slots[0, 0]
    q_max = q_ids.shape[0]
    q_live = jnp.arange(q_max, dtype=jnp.int32) < q_count[0, 0]
    q_row = q_ids // tile_cols
    q_col = q_ids % tile_cols
    zeros_out = jnp.zeros((q_max, 128, 128), jnp.float32)
    p_data = (dense_blocks, p_code)
    s_data = (s_local, s_code)
    level_count = rows_n.bit_length() - 1
    for level in range(level_count):
        moved = jax.tree.map(
            lambda part, own: part.astype(own.dtype),
            shifted(shortened(p_data), "col", -(1 << level)),
            p_data,
        )
        p_data = pick_tree(row_at >> level & 1 == 1, moved, p_data)
    row_offset = col_at % rows_n
    for level in range(level_count):
        moved = jax.tree.map(
            lambda part, own: part.astype(own.dtype),
            shifted(shortened(s_data), "row", -(1 << level)),
            s_data,
        )
        s_data = pick_tree(row_offset >> level & 1 == 1, moved, s_data)

    def advance(step_at, carry):
        summed, p_held, s_held = carry
        panel_at = (row_at + col_at + step_at) % cols_n
        summed = step_product(summed, p_held, s_held, panel_at // rows_n, q_row, q_col, tile_cols)
        p_held = jax.tree.map(
            lambda part, own: part.astype(own.dtype), shifted(shortened(p_held), "col", -1), p_held
        )
        s_held = jax.tree.map(
            lambda part, own: part.astype(own.dtype), shifted(shortened(s_held), "row", -1), s_held
        )
        return (summed, p_held, s_held)

    summed, p_data, s_data = lax.fori_loop(0, cols_n - 1, advance, (zeros_out, p_data, s_data))
    panel_at = (row_at + col_at + cols_n - 1) % cols_n
    summed = step_product(summed, p_data, s_data, panel_at // rows_n, q_row, q_col, tile_cols)
    product = jnp.where(q_live[:, None, None], summed, jnp.zeros_like(summed))
    return (dense_blocks.reshape(1, 1, p_max, 128, 128), product.reshape(1, 1, q_max, 128, 128))


def solution(mesh):
    return jax.shard_map(
        on_device,
        mesh=mesh,
        in_specs=(
            P("row", None),
            P("row", "col", None),
            P("row", "col"),
            P("row", "col", None, None, None),
            P("row", "col", None),
            P("row", "col"),
            P("row", "col", None),
            P("row", "col"),
        ),
        out_specs=(P("row", "col", None, None, None), P("row", "col", None, None, None)),
        check_vma=False,
    )
```

profile of v0, /device:TPU:1, one launch (start us, length us, event | category | flops | bytes accessed | tf_op | source)
XLA Modules:
  0.0 387.4 jit_solution(9958249372721441714)
XLA Ops:
  7.2 2.3 broadcast_select_fusion
  10.7 5.8 %collective-permute-start.12 = (bf16[8,128,128]{2,0,1:T(8,128)(2,1)S(1)}, bf16[8,128,128]{2,0,1:T(8,128)(2,1)S(1)}, u32[]{:S(2)}, u32[]{:S(2)}) collective-permute-start(bf16[8,128,128]{2,0,1:T(8,128)(2,1)S(1)} %bitcast.134), channel_id=1, source_target_pairs={{16,0},{32,16},{48,32},{64,48},{80,64},{96,80},{112,96},{128,112},... | collective-permute-start | bytes 786440 | tf_op jit(solution)/shard_map/ppermute | solution.py:23
  20.4 5.0 %gather_fusion = bf16[8,128,2048]{2,1,0:T(8,128)(2,1)} fusion(bf16[8,128,2048]{2,1,0:T(8,128)(2,1)} %bitcast.131, s32[1024]{0:T(1024)S(1)} %get-tuple-element.386), kind=kCustom, calls=%fused_computation | custom fusion | bytes 8388640 | tf_op jit(solution)/shard_map/gather | solution.py:74
  25.8 8.4 %collective-permute-start.9 = (s32[8]{0:T(128)S(1)}, s32[8]{0:T(128)S(1)}, u32[]{:S(2)}, u32[]{:S(2)}) collective-permute-start(s32[8]{0:T(128)S(1)} %broadcast_select_fusion.13), channel_id=1, source_target_pairs={{2,0},{3,1},{4,2},{5,3},{6,4},{7,5},{8,6},{9,7},{10,8},{11,9},{12,... | collective-permute-start | bytes 104 | tf_op jit(solution)/shard_map/ppermute | solution.py:23
  34.9 2.0 collective-permute-start.10
  36.9 91.7 %all-reduce.2.cloned.1.call-done = bf16[8,128,2048]{2,1,0:T(8,128)(2,1)} async-done(((bf16[8,128,2048]{2,1,0:T(8,128)(2,1)}), bf16[8,128,2048]{2,1,0:T(8,128)(2,1)}) %all-reduce.2.cloned.1.call-update) | async-done | bytes 4194320 | tf_op jit(solution)/shard_map/psum | solution.py:9
  128.6 5.0 %gather_fusion.1 = bf16[8,128,2048]{2,1,0:T(8,128)(2,1)} fusion(bf16[8,128,2048]{2,1,0:T(8,128)(2,1)} %all-reduce.2.cloned.1.call-done, s32[1024]{0:T(1024)S(1)} %get-tuple-element.385), kind=kCustom, calls=%fused_computation.1 | custom fusion | bytes 8388640 | tf_op jit(solution)/shard_map/gather | solution.py:75
  133.6 4.7 %fusion.18 = bf16[8,128,128]{2,1,0:T(8,128)(2,1)S(1)} fusion(bf16[8,128,2048]{2,1,0:T(8,128)(2,1)} %gather_fusion, bf16[8,128,2048]{2,1,0:T(8,128)(2,1)} %gather_fusion.1, pred[8]{0:T(512)(128)(4,1)S(1)} %iota_compare_fusion.5), kind=kOutput, calls=%fused_computation.46 | convolution fusion | flops 537133056 | bytes 8650760 | tf_op jit(solution)/shard_map/pak,pbk->pab/dot_general | solution.py:76
  139.4 2.6 collective-permute-start.19
  142.1 2.3 collective-permute-start.13
  144.6 3.9 %collective-permute-start.5 = (bf16[8,128,128]{2,1,0:T(8,128)(2,1)S(1)}, bf16[8,128,128]{2,1,0:T(8,128)(2,1)S(1)}, u32[]{:S(2)}, u32[]{:S(2)}) collective-permute-start(bf16[8,128,128]{2,1,0:T(8,128)(2,1)S(1)} %broadcast_select_fusion.5), channel_id=1, source_target_pairs={{2,0},{3,1},{4,2},{5,3},{6,4},{7,5},{8,6},{9,7},{10,8},{11,9},{12,... | collective-permute-start | bytes 786440 | tf_op jit(solution)/shard_map/ppermute | solution.py:23
  148.5 3.1 collective-permute-start.11
  151.6 2.7 collective-permute-start.14
  155.6 4.7 %collective-permute-done.14 = bf16[8,128,128]{2,0,1:T(8,128)(2,1)S(1)} collective-permute-done((bf16[8,128,128]{2,0,1:T(8,128)(2,1)S(1)}, bf16[8,128,128]{2,0,1:T(8,128)(2,1)S(1)}, u32[]{:S(2)}, u32[]{:S(2)}) %collective-permute-start.14) | collective-permute-done | bytes 262176 | tf_op jit(solution)/shard_map/ppermute | solution.py:23
  160.3 2.1 collective-permute-start.15
  163.6 4.0 %collective-permute-start.7 = (bf16[8,128,128]{2,1,0:T(8,128)(2,1)S(1)}, bf16[8,128,128]{2,1,0:T(8,128)(2,1)S(1)}, u32[]{:S(2)}, u32[]{:S(2)}) collective-permute-start(bf16[8,128,128]{2,1,0:T(8,128)(2,1)S(1)} %broadcast_select_fusion.7), channel_id=1, source_target_pairs={{8,0},{9,1},{10,2},{11,3},{12,4},{13,5},{14,6},{15,7},{0,8},{1,9},... | collective-permute-start | bytes 786440 | tf_op jit(solution)/shard_map/ppermute | solution.py:23
  167.6 1.9 collective-permute-done.15
  169.5 9.9 %collective-permute-done.7 = bf16[8,128,128]{2,1,0:T(8,128)(2,1)S(1)} collective-permute-done((bf16[8,128,128]{2,1,0:T(8,128)(2,1)S(1)}, bf16[8,128,128]{2,1,0:T(8,128)(2,1)S(1)}, u32[]{:S(2)}, u32[]{:S(2)}) %collective-permute-start.7) | collective-permute-done | bytes 262176 | tf_op jit(solution)/shard_map/ppermute | solution.py:23
  179.6 191.7 %while.25 = (s32[]{:T(128)}, f32[8,128,128]{2,1,0:T(8,128)}, bf16[8,128,128]{2,0,1:T(8,128)(2,1)S(1)}, s32[8]{0:T(128)S(1)}, bf16[8,128,128]{2,0,1:T(8,128)(2,1)...) while((s32[]{:T(128)}, f32[8,128,128]{2,1,0:T(8,128)}, ...), condition=%wide.region_2.3_spmd.clone, body=%wide.region_1.2_spmd.clone.sunk | while | flops 304351008 | bytes 25692068 | solution.py:121
  179.7 2.0 collective-permute-start
  181.6 5.7 %collective-permute-start.2 = (bf16[8,128,128]{2,0,1:T(8,128)(2,1)S(1)}, bf16[8,128,128]{2,0,1:T(8,128)(2,1)S(1)}, u32[]{:S(2)}, u32[]{:S(2)}) collective-permute-start(bf16[8,128,128]{2,0,1:T(8,128)(2,1)S(1)} %copy.49), channel_id=1, source_target_pairs={{16,0},{32,16},{48,32},{64,48},{80,64},{96,80},{112,96},{128,112},... | collective-permute-start | bytes 786440 | tf_op jit(solution)/shard_map/while/body/eval_jaxpr/ppermute | solution.py:23
  187.4 4.8 %collective-permute-start.1 = (s32[8]{0:T(128)S(1)}, s32[8]{0:T(128)S(1)}, u32[]{:S(2)}, u32[]{:S(2)}) collective-permute-start(s32[8]{0:T(128)S(1)} %copy.48), channel_id=1, source_target_pairs={{1,0},{2,1},{3,2},{4,3},{5,4},{6,5},{7,6},{8,7},{9,8},{10,9},{11,1... | collective-permute-start | bytes 104 | tf_op jit(solution)/shard_map/while/body/eval_jaxpr/ppermute | solution.py:23
  194.5 2.3 reshape.448
  202.2 1.9 collective-permute-start.1
  205.0 2.3 reshape.448
  208.9 2.8 fusion.49
  214.5 1.9 collective-permute-start.1
  217.2 2.3 reshape.448
  221.1 2.8 fusion.49
  226.8 1.9 collective-permute-start.1
  229.5 2.3 reshape.448
  233.4 2.8 fusion.49
  239.1 1.9 collective-permute-start.1
  241.8 2.3 reshape.448
  245.7 2.8 fusion.49
  251.3 1.9 collective-permute-start.1
  254.1 2.3 reshape.448
  258.0 2.8 fusion.49
  263.6 1.9 collective-permute-start.1
  266.4 2.3 reshape.448
  270.3 2.8 fusion.49
  275.9 1.9 collective-permute-start.1
  278.6 2.3 reshape.448
  282.5 2.8 fusion.49
  288.2 1.9 collective-permute-start.1
  290.9 2.3 reshape.448
  294.8 2.8 fusion.49
  300.4 1.9 collective-permute-start.1
  303.2 2.3 reshape.448
  307.1 2.8 fusion.49
  312.7 1.9 collective-permute-start.1
  315.5 2.3 reshape.448
  319.4 2.8 fusion.49
  325.0 1.9 collective-permute-start.1
  327.7 2.3 reshape.448
  331.6 2.8 fusion.49
  340.0 2.3 reshape.448
  343.9 2.8 fusion.49
  352.3 2.3 reshape.448
  356.2 2.8 fusion.49
  364.6 2.3 reshape.448
  368.5 2.8 fusion.49
  372.1 2.3 reshape.418
  376.8 2.8 fusion.15
  (390 shorter events, 95.0 us)
Async XLA Ops:
  7.2 121.4 %all-reduce.2.cloned.1.call-start = ((), (), s32[]{:S(2)}) async-start(), calls=%async_computation | async-start | bytes 8388608 | tf_op jit(solution)/shard_map/psum | solution.py:9
  10.7 131.3 %collective-permute-start.12 = (bf16[8,128,128]{2,0,1:T(8,128)(2,1)S(1)}, bf16[8,128,128]{2,0,1:T(8,128)(2,1)S(1)}, u32[]{:S(2)}, u32[]{:S(2)}) collective-permute-start(bf16[8,128,128]{2,0,1:T(8,128)(2,1)S(1)} %bitcast.134), channel_id=1, source_target_pairs={{16,0},{32,16},{48,32},{64,48},{80,64},{96,80},{112,96},{128,112},... | collective-permute-start | bytes 786440 | tf_op jit(solution)/shard_map/ppermute | solution.py:23
  17.2 8.3 %collective-permute-start.16 = (s32[8]{0:T(128)S(1)}, s32[8]{0:T(128)S(1)}, u32[]{:S(2)}, u32[]{:S(2)}) collective-permute-start(s32[8]{0:T(128)S(1)} %compare_select_fusion.15), channel_id=1, source_target_pairs={{16,0},{32,16},{48,32},{64,48},{80,64},{96,80},{112,96},{128,112},... | collective-permute-start | bytes 104 | tf_op jit(solution)/shard_map/ppermute | solution.py:23
  25.5 8.7 %collective-permute-start.17 = (s32[8]{0:T(128)S(1)}, s32[8]{0:T(128)S(1)}, u32[]{:S(2)}, u32[]{:S(2)}) collective-permute-start(s32[8]{0:T(128)S(1)} %broadcast_select_fusion.9), channel_id=1, source_target_pairs={{32,0},{48,16},{64,32},{80,48},{96,64},{112,80},{128,96},{144,112}... | collective-permute-start | bytes 104 | tf_op jit(solution)/shard_map/ppermute | solution.py:23
  25.8 9.1 %collective-permute-start.9 = (s32[8]{0:T(128)S(1)}, s32[8]{0:T(128)S(1)}, u32[]{:S(2)}, u32[]{:S(2)}) collective-permute-start(s32[8]{0:T(128)S(1)} %broadcast_select_fusion.13), channel_id=1, source_target_pairs={{2,0},{3,1},{4,2},{5,3},{6,4},{7,5},{8,6},{9,7},{10,8},{11,9},{12,... | collective-permute-start | bytes 104 | tf_op jit(solution)/shard_map/ppermute | solution.py:23
  34.2 105.2 %collective-permute-start.18 = (s32[8]{0:T(128)S(1)}, s32[8]{0:T(128)S(1)}, u32[]{:S(2)}, u32[]{:S(2)}) collective-permute-start(s32[8]{0:T(128)S(1)} %broadcast_select_fusion.10), channel_id=1, source_target_pairs={{64,0},{80,16},{96,32},{112,48},{128,64},{144,80},{160,96},{176,11... | collective-permute-start | bytes 104 | tf_op jit(solution)/shard_map/ppermute | solution.py:23
  34.9 113.6 %collective-permute-start.10 = (s32[8]{0:T(128)S(1)}, s32[8]{0:T(128)S(1)}, u32[]{:S(2)}, u32[]{:S(2)}) collective-permute-start(s32[8]{0:T(128)S(1)} %broadcast_select_fusion.14), channel_id=1, source_target_pairs={{4,0},{5,1},{6,2},{7,3},{8,4},{9,5},{10,6},{11,7},{12,8},{13,9},{1... | collective-permute-start | bytes 104 | tf_op jit(solution)/shard_map/ppermute | solution.py:23
  139.4 16.2 %collective-permute-start.19 = (s32[8]{0:T(128)S(1)}, s32[8]{0:T(128)S(1)}, u32[]{:S(2)}, u32[]{:S(2)}) collective-permute-start(s32[8]{0:T(128)S(1)} %broadcast_select_fusion.11), channel_id=1, source_target_pairs={{128,0},{144,16},{160,32},{176,48},{192,64},{208,80},{224,96},{240... | collective-permute-start | bytes 104 | tf_op jit(solution)/shard_map/ppermute | solution.py:23
  142.1 9.5 %collective-permute-start.13 = (bf16[8,128,128]{2,0,1:T(8,128)(2,1)S(1)}, bf16[8,128,128]{2,0,1:T(8,128)(2,1)S(1)}, u32[]{:S(2)}, u32[]{:S(2)}) collective-permute-start(bf16[8,128,128]{2,0,1:T(8,128)(2,1)S(1)} %broadcast_select_fusion.1), channel_id=1, source_target_pairs={{32,0},{48,16},{64,32},{80,48},{96,64},{112,80},{128,96},{144,112}... | collective-permute-start | bytes 786440 | tf_op jit(solution)/shard_map/ppermute | solution.py:23
  144.6 9.6 %collective-permute-start.5 = (bf16[8,128,128]{2,1,0:T(8,128)(2,1)S(1)}, bf16[8,128,128]{2,1,0:T(8,128)(2,1)S(1)}, u32[]{:S(2)}, u32[]{:S(2)}) collective-permute-start(bf16[8,128,128]{2,1,0:T(8,128)(2,1)S(1)} %broadcast_select_fusion.5), channel_id=1, source_target_pairs={{2,0},{3,1},{4,2},{5,3},{6,4},{7,5},{8,6},{9,7},{10,8},{11,9},{12,... | collective-permute-start | bytes 786440 | tf_op jit(solution)/shard_map/ppermute | solution.py:23
  148.5 19.0 %collective-permute-start.11 = (s32[8]{0:T(128)S(1)}, s32[8]{0:T(128)S(1)}, u32[]{:S(2)}, u32[]{:S(2)}) collective-permute-start(s32[8]{0:T(128)S(1)} %broadcast_select_fusion.15), channel_id=1, source_target_pairs={{8,0},{9,1},{10,2},{11,3},{12,4},{13,5},{14,6},{15,7},{0,8},{1,9},... | collective-permute-start | bytes 104 | tf_op jit(solution)/shard_map/ppermute | solution.py:23
  151.6 8.7 %collective-permute-start.14 = (bf16[8,128,128]{2,0,1:T(8,128)(2,1)S(1)}, bf16[8,128,128]{2,0,1:T(8,128)(2,1)S(1)}, u32[]{:S(2)}, u32[]{:S(2)}) collective-permute-start(bf16[8,128,128]{2,0,1:T(8,128)(2,1)S(1)} %broadcast_select_fusion.2), channel_id=1, source_target_pairs={{64,0},{80,16},{96,32},{112,48},{128,64},{144,80},{160,96},{176,11... | collective-permute-start | bytes 786440 | tf_op jit(solution)/shard_map/ppermute | solution.py:23
  154.3 9.2 %collective-permute-start.6 = (bf16[8,128,128]{2,1,0:T(8,128)(2,1)S(1)}, bf16[8,128,128]{2,1,0:T(8,128)(2,1)S(1)}, u32[]{:S(2)}, u32[]{:S(2)}) collective-permute-start(bf16[8,128,128]{2,1,0:T(8,128)(2,1)S(1)} %broadcast_select_fusion.6), channel_id=1, source_target_pairs={{4,0},{5,1},{6,2},{7,3},{8,4},{9,5},{10,6},{11,7},{12,8},{13,9},{1... | collective-permute-start | bytes 786440 | tf_op jit(solution)/shard_map/ppermute | solution.py:23
  160.3 9.1 %collective-permute-start.15 = (bf16[8,128,128]{2,0,1:T(8,128)(2,1)S(1)}, bf16[8,128,128]{2,0,1:T(8,128)(2,1)S(1)}, u32[]{:S(2)}, u32[]{:S(2)}) collective-permute-start(bf16[8,128,128]{2,0,1:T(8,128)(2,1)S(1)} %broadcast_select_fusion.3), channel_id=1, source_target_pairs={{128,0},{144,16},{160,32},{176,48},{192,64},{208,80},{224,96},{240... | collective-permute-start | bytes 786440 | tf_op jit(solution)/shard_map/ppermute | solution.py:23
  163.6 15.8 %collective-permute-start.7 = (bf16[8,128,128]{2,1,0:T(8,128)(2,1)S(1)}, bf16[8,128,128]{2,1,0:T(8,128)(2,1)S(1)}, u32[]{:S(2)}, u32[]{:S(2)}) collective-permute-start(bf16[8,128,128]{2,1,0:T(8,128)(2,1)S(1)} %broadcast_select_fusion.7), channel_id=1, source_target_pairs={{8,0},{9,1},{10,2},{11,3},{12,4},{13,5},{14,6},{15,7},{0,8},{1,9},... | collective-permute-start | bytes 786440 | tf_op jit(solution)/shard_map/ppermute | solution.py:23
  179.7 20.5 %collective-permute-start = (bf16[8,128,128]{2,0,1:T(8,128)(2,1)S(1)}, bf16[8,128,128]{2,0,1:T(8,128)(2,1)S(1)}, u32[]{:S(2)}, u32[]{:S(2)}) collective-permute-start(bf16[8,128,128]{2,0,1:T(8,128)(2,1)S(1)} %copy.47), channel_id=1, source_target_pairs={{1,0},{2,1},{3,2},{4,3},{5,4},{6,5},{7,6},{8,7},{9,8},{10,9},{11,1... | collective-permute-start | bytes 786440 | tf_op jit(solution)/shard_map/while/body/eval_jaxpr/ppermute | solution.py:23
  181.6 18.6 %collective-permute-start.2 = (bf16[8,128,128]{2,0,1:T(8,128)(2,1)S(1)}, bf16[8,128,128]{2,0,1:T(8,128)(2,1)S(1)}, u32[]{:S(2)}, u32[]{:S(2)}) collective-permute-start(bf16[8,128,128]{2,0,1:T(8,128)(2,1)S(1)} %copy.49), channel_id=1, source_target_pairs={{16,0},{32,16},{48,32},{64,48},{80,64},{96,80},{112,96},{128,112},... | collective-permute-start | bytes 786440 | tf_op jit(solution)/shard_map/while/body/eval_jaxpr/ppermute | solution.py:23
  187.4 12.8 %collective-permute-start.1 = (s32[8]{0:T(128)S(1)}, s32[8]{0:T(128)S(1)}, u32[]{:S(2)}, u32[]{:S(2)}) collective-permute-start(s32[8]{0:T(128)S(1)} %copy.48), channel_id=1, source_target_pairs={{1,0},{2,1},{3,2},{4,3},{5,4},{6,5},{7,6},{8,7},{9,8},{10,9},{11,1... | collective-permute-start | bytes 104 | tf_op jit(solution)/shard_map/while/body/eval_jaxpr/ppermute | solution.py:23
  192.2 8.0 %collective-permute-start.3 = (s32[8]{0:T(128)S(1)}, s32[8]{0:T(128)S(1)}, u32[]{:S(2)}, u32[]{:S(2)}) collective-permute-start(s32[8]{0:T(128)S(1)} %copy.50), channel_id=1, source_target_pairs={{16,0},{32,16},{48,32},{64,48},{80,64},{96,80},{112,96},{128,112},... | collective-permute-start | bytes 104 | tf_op jit(solution)/shard_map/while/body/eval_jaxpr/ppermute | solution.py:23
  200.3 11.4 %collective-permute-start = (bf16[8,128,128]{2,0,1:T(8,128)(2,1)S(1)}, bf16[8,128,128]{2,0,1:T(8,128)(2,1)S(1)}, u32[]{:S(2)}, u32[]{:S(2)}) collective-permute-start(bf16[8,128,128]{2,0,1:T(8,128)(2,1)S(1)} %copy.47), channel_id=1, source_target_pairs={{1,0},{2,1},{3,2},{4,3},{5,4},{6,5},{7,6},{8,7},{9,8},{10,9},{11,1... | collective-permute-start | bytes 786440 | tf_op jit(solution)/shard_map/while/body/eval_jaxpr/ppermute | solution.py:23
  200.9 10.8 %collective-permute-start.2 = (bf16[8,128,128]{2,0,1:T(8,128)(2,1)S(1)}, bf16[8,128,128]{2,0,1:T(8,128)(2,1)S(1)}, u32[]{:S(2)}, u32[]{:S(2)}) collective-permute-start(bf16[8,128,128]{2,0,1:T(8,128)(2,1)S(1)} %copy.49), channel_id=1, source_target_pairs={{16,0},{32,16},{48,32},{64,48},{80,64},{96,80},{112,96},{128,112},... | collective-permute-start | bytes 786440 | tf_op jit(solution)/shard_map/while/body/eval_jaxpr/ppermute | solution.py:23
  202.2 9.5 %collective-permute-start.1 = (s32[8]{0:T(128)S(1)}, s32[8]{0:T(128)S(1)}, u32[]{:S(2)}, u32[]{:S(2)}) collective-permute-start(s32[8]{0:T(128)S(1)} %copy.48), channel_id=1, source_target_pairs={{1,0},{2,1},{3,2},{4,3},{5,4},{6,5},{7,6},{8,7},{9,8},{10,9},{11,1... | collective-permute-start | bytes 104 | tf_op jit(solution)/shard_map/while/body/eval_jaxpr/ppermute | solution.py:23
  211.8 12.2 %collective-permute-start = (bf16[8,128,128]{2,0,1:T(8,128)(2,1)S(1)}, bf16[8,128,128]{2,0,1:T(8,128)(2,1)S(1)}, u32[]{:S(2)}, u32[]{:S(2)}) collective-permute-start(bf16[8,128,128]{2,0,1:T(8,128)(2,1)S(1)} %copy.47), channel_id=1, source_target_pairs={{1,0},{2,1},{3,2},{4,3},{5,4},{6,5},{7,6},{8,7},{9,8},{10,9},{11,1... | collective-permute-start | bytes 786440 | tf_op jit(solution)/shard_map/while/body/eval_jaxpr/ppermute | solution.py:23
  212.8 11.2 %collective-permute-start.2 = (bf16[8,128,128]{2,0,1:T(8,128)(2,1)S(1)}, bf16[8,128,128]{2,0,1:T(8,128)(2,1)S(1)}, u32[]{:S(2)}, u32[]{:S(2)}) collective-permute-start(bf16[8,128,128]{2,0,1:T(8,128)(2,1)S(1)} %copy.49), channel_id=1, source_target_pairs={{16,0},{32,16},{48,32},{64,48},{80,64},{96,80},{112,96},{128,112},... | collective-permute-start | bytes 786440 | tf_op jit(solution)/shard_map/while/body/eval_jaxpr/ppermute | solution.py:23
  214.5 9.5 %collective-permute-start.1 = (s32[8]{0:T(128)S(1)}, s32[8]{0:T(128)S(1)}, u32[]{:S(2)}, u32[]{:S(2)}) collective-permute-start(s32[8]{0:T(128)S(1)} %copy.48), channel_id=1, source_target_pairs={{1,0},{2,1},{3,2},{4,3},{5,4},{6,5},{7,6},{8,7},{9,8},{10,9},{11,1... | collective-permute-start | bytes 104 | tf_op jit(solution)/shard_map/while/body/eval_jaxpr/ppermute | solution.py:23
  224.0 12.2 %collective-permute-start = (bf16[8,128,128]{2,0,1:T(8,128)(2,1)S(1)}, bf16[8,128,128]{2,0,1:T(8,128)(2,1)S(1)}, u32[]{:S(2)}, u32[]{:S(2)}) collective-permute-start(bf16[8,128,128]{2,0,1:T(8,128)(2,1)S(1)} %copy.47), channel_id=1, source_target_pairs={{1,0},{2,1},{3,2},{4,3},{5,4},{6,5},{7,6},{8,7},{9,8},{10,9},{11,1... | collective-permute-start | bytes 786440 | tf_op jit(solution)/shard_map/while/body/eval_jaxpr/ppermute | solution.py:23
  225.1 11.2 %collective-permute-start.2 = (bf16[8,128,128]{2,0,1:T(8,128)(2,1)S(1)}, bf16[8,128,128]{2,0,1:T(8,128)(2,1)S(1)}, u32[]{:S(2)}, u32[]{:S(2)}) collective-permute-start(bf16[8,128,128]{2,0,1:T(8,128)(2,1)S(1)} %copy.49), channel_id=1, source_target_pairs={{16,0},{32,16},{48,32},{64,48},{80,64},{96,80},{112,96},{128,112},... | collective-permute-start | bytes 786440 | tf_op jit(solution)/shard_map/while/body/eval_jaxpr/ppermute | solution.py:23
  226.8 9.5 %collective-permute-start.1 = (s32[8]{0:T(128)S(1)}, s32[8]{0:T(128)S(1)}, u32[]{:S(2)}, u32[]{:S(2)}) collective-permute-start(s32[8]{0:T(128)S(1)} %copy.48), channel_id=1, source_target_pairs={{1,0},{2,1},{3,2},{4,3},{5,4},{6,5},{7,6},{8,7},{9,8},{10,9},{11,1... | collective-permute-start | bytes 104 | tf_op jit(solution)/shard_map/while/body/eval_jaxpr/ppermute | solution.py:23
  236.3 12.2 %collective-permute-start = (bf16[8,128,128]{2,0,1:T(8,128)(2,1)S(1)}, bf16[8,128,128]{2,0,1:T(8,128)(2,1)S(1)}, u32[]{:S(2)}, u32[]{:S(2)}) collective-permute-start(bf16[8,128,128]{2,0,1:T(8,128)(2,1)S(1)} %copy.47), channel_id=1, source_target_pairs={{1,0},{2,1},{3,2},{4,3},{5,4},{6,5},{7,6},{8,7},{9,8},{10,9},{11,1... | collective-permute-start | bytes 786440 | tf_op jit(solution)/shard_map/while/body/eval_jaxpr/ppermute | solution.py:23
  237.3 11.2 %collective-permute-start.2 = (bf16[8,128,128]{2,0,1:T(8,128)(2,1)S(1)}, bf16[8,128,128]{2,0,1:T(8,128)(2,1)S(1)}, u32[]{:S(2)}, u32[]{:S(2)}) collective-permute-start(bf16[8,128,128]{2,0,1:T(8,128)(2,1)S(1)} %copy.49), channel_id=1, source_target_pairs={{16,0},{32,16},{48,32},{64,48},{80,64},{96,80},{112,96},{128,112},... | collective-permute-start | bytes 786440 | tf_op jit(solution)/shard_map/while/body/eval_jaxpr/ppermute | solution.py:23
  239.1 9.5 %collective-permute-start.1 = (s32[8]{0:T(128)S(1)}, s32[8]{0:T(128)S(1)}, u32[]{:S(2)}, u32[]{:S(2)}) collective-permute-start(s32[8]{0:T(128)S(1)} %copy.48), channel_id=1, source_target_pairs={{1,0},{2,1},{3,2},{4,3},{5,4},{6,5},{7,6},{8,7},{9,8},{10,9},{11,1... | collective-permute-start | bytes 104 | tf_op jit(solution)/shard_map/while/body/eval_jaxpr/ppermute | solution.py:23
  248.6 12.2 %collective-permute-start = (bf16[8,128,128]{2,0,1:T(8,128)(2,1)S(1)}, bf16[8,128,128]{2,0,1:T(8,128)(2,1)S(1)}, u32[]{:S(2)}, u32[]{:S(2)}) collective-permute-start(bf16[8,128,128]{2,0,1:T(8,128)(2,1)S(1)} %copy.47), channel_id=1, source_target_pairs={{1,0},{2,1},{3,2},{4,3},{5,4},{6,5},{7,6},{8,7},{9,8},{10,9},{11,1... | collective-permute-start | bytes 786440 | tf_op jit(solution)/shard_map/while/body/eval_jaxpr/ppermute | solution.py:23
  249.6 11.2 %collective-permute-start.2 = (bf16[8,128,128]{2,0,1:T(8,128)(2,1)S(1)}, bf16[8,128,128]{2,0,1:T(8,128)(2,1)S(1)}, u32[]{:S(2)}, u32[]{:S(2)}) collective-permute-start(bf16[8,128,128]{2,0,1:T(8,128)(2,1)S(1)} %copy.49), channel_id=1, source_target_pairs={{16,0},{32,16},{48,32},{64,48},{80,64},{96,80},{112,96},{128,112},... | collective-permute-start | bytes 786440 | tf_op jit(solution)/shard_map/while/body/eval_jaxpr/ppermute | solution.py:23
  251.3 9.5 %collective-permute-start.1 = (s32[8]{0:T(128)S(1)}, s32[8]{0:T(128)S(1)}, u32[]{:S(2)}, u32[]{:S(2)}) collective-permute-start(s32[8]{0:T(128)S(1)} %copy.48), channel_id=1, source_target_pairs={{1,0},{2,1},{3,2},{4,3},{5,4},{6,5},{7,6},{8,7},{9,8},{10,9},{11,1... | collective-permute-start | bytes 104 | tf_op jit(solution)/shard_map/while/body/eval_jaxpr/ppermute | solution.py:23
  253.2 7.6 %collective-permute-start.3 = (s32[8]{0:T(128)S(1)}, s32[8]{0:T(128)S(1)}, u32[]{:S(2)}, u32[]{:S(2)}) collective-permute-start(s32[8]{0:T(128)S(1)} %copy.50), channel_id=1, source_target_pairs={{16,0},{32,16},{48,32},{64,48},{80,64},{96,80},{112,96},{128,112},... | collective-permute-start | bytes 104 | tf_op jit(solution)/shard_map/while/body/eval_jaxpr/ppermute | solution.py:23
  260.9 12.2 %collective-permute-start = (bf16[8,128,128]{2,0,1:T(8,128)(2,1)S(1)}, bf16[8,128,128]{2,0,1:T(8,128)(2,1)S(1)}, u32[]{:S(2)}, u32[]{:S(2)}) collective-permute-start(bf16[8,128,128]{2,0,1:T(8,128)(2,1)S(1)} %copy.47), channel_id=1, source_target_pairs={{1,0},{2,1},{3,2},{4,3},{5,4},{6,5},{7,6},{8,7},{9,8},{10,9},{11,1... | collective-permute-start | bytes 786440 | tf_op jit(solution)/shard_map/while/body/eval_jaxpr/ppermute | solution.py:23
  261.9 11.2 %collective-permute-start.2 = (bf16[8,128,128]{2,0,1:T(8,128)(2,1)S(1)}, bf16[8,128,128]{2,0,1:T(8,128)(2,1)S(1)}, u32[]{:S(2)}, u32[]{:S(2)}) collective-permute-start(bf16[8,128,128]{2,0,1:T(8,128)(2,1)S(1)} %copy.49), channel_id=1, source_target_pairs={{16,0},{32,16},{48,32},{64,48},{80,64},{96,80},{112,96},{128,112},... | collective-permute-start | bytes 786440 | tf_op jit(solution)/shard_map/while/body/eval_jaxpr/ppermute | solution.py:23
  263.6 9.5 %collective-permute-start.1 = (s32[8]{0:T(128)S(1)}, s32[8]{0:T(128)S(1)}, u32[]{:S(2)}, u32[]{:S(2)}) collective-permute-start(s32[8]{0:T(128)S(1)} %copy.48), channel_id=1, source_target_pairs={{1,0},{2,1},{3,2},{4,3},{5,4},{6,5},{7,6},{8,7},{9,8},{10,9},{11,1... | collective-permute-start | bytes 104 | tf_op jit(solution)/shard_map/while/body/eval_jaxpr/ppermute | solution.py:23
  265.5 7.6 %collective-permute-start.3 = (s32[8]{0:T(128)S(1)}, s32[8]{0:T(128)S(1)}, u32[]{:S(2)}, u32[]{:S(2)}) collective-permute-start(s32[8]{0:T(128)S(1)} %copy.50), channel_id=1, source_target_pairs={{16,0},{32,16},{48,32},{64,48},{80,64},{96,80},{112,96},{128,112},... | collective-permute-start | bytes 104 | tf_op jit(solution)/shard_map/while/body/eval_jaxpr/ppermute | solution.py:23
  273.1 12.2 %collective-permute-start = (bf16[8,128,128]{2,0,1:T(8,128)(2,1)S(1)}, bf16[8,128,128]{2,0,1:T(8,128)(2,1)S(1)}, u32[]{:S(2)}, u32[]{:S(2)}) collective-permute-start(bf16[8,128,128]{2,0,1:T(8,128)(2,1)S(1)} %copy.47), channel_id=1, source_target_pairs={{1,0},{2,1},{3,2},{4,3},{5,4},{6,5},{7,6},{8,7},{9,8},{10,9},{11,1... | collective-permute-start | bytes 786440 | tf_op jit(solution)/shard_map/while/body/eval_jaxpr/ppermute | solution.py:23
  274.2 11.2 %collective-permute-start.2 = (bf16[8,128,128]{2,0,1:T(8,128)(2,1)S(1)}, bf16[8,128,128]{2,0,1:T(8,128)(2,1)S(1)}, u32[]{:S(2)}, u32[]{:S(2)}) collective-permute-start(bf16[8,128,128]{2,0,1:T(8,128)(2,1)S(1)} %copy.49), channel_id=1, source_target_pairs={{16,0},{32,16},{48,32},{64,48},{80,64},{96,80},{112,96},{128,112},... | collective-permute-start | bytes 786440 | tf_op jit(solution)/shard_map/while/body/eval_jaxpr/ppermute | solution.py:23
  275.9 9.5 %collective-permute-start.1 = (s32[8]{0:T(128)S(1)}, s32[8]{0:T(128)S(1)}, u32[]{:S(2)}, u32[]{:S(2)}) collective-permute-start(s32[8]{0:T(128)S(1)} %copy.48), channel_id=1, source_target_pairs={{1,0},{2,1},{3,2},{4,3},{5,4},{6,5},{7,6},{8,7},{9,8},{10,9},{11,1... | collective-permute-start | bytes 104 | tf_op jit(solution)/shard_map/while/body/eval_jaxpr/ppermute | solution.py:23
  285.4 12.2 %collective-permute-start = (bf16[8,128,128]{2,0,1:T(8,128)(2,1)S(1)}, bf16[8,128,128]{2,0,1:T(8,128)(2,1)S(1)}, u32[]{:S(2)}, u32[]{:S(2)}) collective-permute-start(bf16[8,128,128]{2,0,1:T(8,128)(2,1)S(1)} %copy.47), channel_id=1, source_target_pairs={{1,0},{2,1},{3,2},{4,3},{5,4},{6,5},{7,6},{8,7},{9,8},{10,9},{11,1... | collective-permute-start | bytes 786440 | tf_op jit(solution)/shard_map/while/body/eval_jaxpr/ppermute | solution.py:23
  286.4 11.2 %collective-permute-start.2 = (bf16[8,128,128]{2,0,1:T(8,128)(2,1)S(1)}, bf16[8,128,128]{2,0,1:T(8,128)(2,1)S(1)}, u32[]{:S(2)}, u32[]{:S(2)}) collective-permute-start(bf16[8,128,128]{2,0,1:T(8,128)(2,1)S(1)} %copy.49), channel_id=1, source_target_pairs={{16,0},{32,16},{48,32},{64,48},{80,64},{96,80},{112,96},{128,112},... | collective-permute-start | bytes 786440 | tf_op jit(solution)/shard_map/while/body/eval_jaxpr/ppermute | solution.py:23
  288.2 9.5 %collective-permute-start.1 = (s32[8]{0:T(128)S(1)}, s32[8]{0:T(128)S(1)}, u32[]{:S(2)}, u32[]{:S(2)}) collective-permute-start(s32[8]{0:T(128)S(1)} %copy.48), channel_id=1, source_target_pairs={{1,0},{2,1},{3,2},{4,3},{5,4},{6,5},{7,6},{8,7},{9,8},{10,9},{11,1... | collective-permute-start | bytes 104 | tf_op jit(solution)/shard_map/while/body/eval_jaxpr/ppermute | solution.py:23
  297.7 12.2 %collective-permute-start = (bf16[8,128,128]{2,0,1:T(8,128)(2,1)S(1)}, bf16[8,128,128]{2,0,1:T(8,128)(2,1)S(1)}, u32[]{:S(2)}, u32[]{:S(2)}) collective-permute-start(bf16[8,128,128]{2,0,1:T(8,128)(2,1)S(1)} %copy.47), channel_id=1, source_target_pairs={{1,0},{2,1},{3,2},{4,3},{5,4},{6,5},{7,6},{8,7},{9,8},{10,9},{11,1... | collective-permute-start | bytes 786440 | tf_op jit(solution)/shard_map/while/body/eval_jaxpr/ppermute | solution.py:23
  298.7 11.2 %collective-permute-start.2 = (bf16[8,128,128]{2,0,1:T(8,128)(2,1)S(1)}, bf16[8,128,128]{2,0,1:T(8,128)(2,1)S(1)}, u32[]{:S(2)}, u32[]{:S(2)}) collective-permute-start(bf16[8,128,128]{2,0,1:T(8,128)(2,1)S(1)} %copy.49), channel_id=1, source_target_pairs={{16,0},{32,16},{48,32},{64,48},{80,64},{96,80},{112,96},{128,112},... | collective-permute-start | bytes 786440 | tf_op jit(solution)/shard_map/while/body/eval_jaxpr/ppermute | solution.py:23
  300.4 9.5 %collective-permute-start.1 = (s32[8]{0:T(128)S(1)}, s32[8]{0:T(128)S(1)}, u32[]{:S(2)}, u32[]{:S(2)}) collective-permute-start(s32[8]{0:T(128)S(1)} %copy.48), channel_id=1, source_target_pairs={{1,0},{2,1},{3,2},{4,3},{5,4},{6,5},{7,6},{8,7},{9,8},{10,9},{11,1... | collective-permute-start | bytes 104 | tf_op jit(solution)/shard_map/while/body/eval_jaxpr/ppermute | solution.py:23
  302.3 7.6 %collective-permute-start.3 = (s32[8]{0:T(128)S(1)}, s32[8]{0:T(128)S(1)}, u32[]{:S(2)}, u32[]{:S(2)}) collective-permute-start(s32[8]{0:T(128)S(1)} %copy.50), channel_id=1, source_target_pairs={{16,0},{32,16},{48,32},{64,48},{80,64},{96,80},{112,96},{128,112},... | collective-permute-start | bytes 104 | tf_op jit(solution)/shard_map/while/body/eval_jaxpr/ppermute | solution.py:23
  310.0 12.2 %collective-permute-start = (bf16[8,128,128]{2,0,1:T(8,128)(2,1)S(1)}, bf16[8,128,128]{2,0,1:T(8,128)(2,1)S(1)}, u32[]{:S(2)}, u32[]{:S(2)}) collective-permute-start(bf16[8,128,128]{2,0,1:T(8,128)(2,1)S(1)} %copy.47), channel_id=1, source_target_pairs={{1,0},{2,1},{3,2},{4,3},{5,4},{6,5},{7,6},{8,7},{9,8},{10,9},{11,1... | collective-permute-start | bytes 786440 | tf_op jit(solution)/shard_map/while/body/eval_jaxpr/ppermute | solution.py:23
  311.0 11.2 %collective-permute-start.2 = (bf16[8,128,128]{2,0,1:T(8,128)(2,1)S(1)}, bf16[8,128,128]{2,0,1:T(8,128)(2,1)S(1)}, u32[]{:S(2)}, u32[]{:S(2)}) collective-permute-start(bf16[8,128,128]{2,0,1:T(8,128)(2,1)S(1)} %copy.49), channel_id=1, source_target_pairs={{16,0},{32,16},{48,32},{64,48},{80,64},{96,80},{112,96},{128,112},... | collective-permute-start | bytes 786440 | tf_op jit(solution)/shard_map/while/body/eval_jaxpr/ppermute | solution.py:23
  312.7 9.5 %collective-permute-start.1 = (s32[8]{0:T(128)S(1)}, s32[8]{0:T(128)S(1)}, u32[]{:S(2)}, u32[]{:S(2)}) collective-permute-start(s32[8]{0:T(128)S(1)} %copy.48), channel_id=1, source_target_pairs={{1,0},{2,1},{3,2},{4,3},{5,4},{6,5},{7,6},{8,7},{9,8},{10,9},{11,1... | collective-permute-start | bytes 104 | tf_op jit(solution)/shard_map/while/body/eval_jaxpr/ppermute | solution.py:23
  322.2 12.2 %collective-permute-start = (bf16[8,128,128]{2,0,1:T(8,128)(2,1)S(1)}, bf16[8,128,128]{2,0,1:T(8,128)(2,1)S(1)}, u32[]{:S(2)}, u32[]{:S(2)}) collective-permute-start(bf16[8,128,128]{2,0,1:T(8,128)(2,1)S(1)} %copy.47), channel_id=1, source_target_pairs={{1,0},{2,1},{3,2},{4,3},{5,4},{6,5},{7,6},{8,7},{9,8},{10,9},{11,1... | collective-permute-start | bytes 786440 | tf_op jit(solution)/shard_map/while/body/eval_jaxpr/ppermute | solution.py:23
  323.3 11.2 %collective-permute-start.2 = (bf16[8,128,128]{2,0,1:T(8,128)(2,1)S(1)}, bf16[8,128,128]{2,0,1:T(8,128)(2,1)S(1)}, u32[]{:S(2)}, u32[]{:S(2)}) collective-permute-start(bf16[8,128,128]{2,0,1:T(8,128)(2,1)S(1)} %copy.49), channel_id=1, source_target_pairs={{16,0},{32,16},{48,32},{64,48},{80,64},{96,80},{112,96},{128,112},... | collective-permute-start | bytes 786440 | tf_op jit(solution)/shard_map/while/body/eval_jaxpr/ppermute | solution.py:23
  325.0 9.5 %collective-permute-start.1 = (s32[8]{0:T(128)S(1)}, s32[8]{0:T(128)S(1)}, u32[]{:S(2)}, u32[]{:S(2)}) collective-permute-start(s32[8]{0:T(128)S(1)} %copy.48), channel_id=1, source_target_pairs={{1,0},{2,1},{3,2},{4,3},{5,4},{6,5},{7,6},{8,7},{9,8},{10,9},{11,1... | collective-permute-start | bytes 104 | tf_op jit(solution)/shard_map/while/body/eval_jaxpr/ppermute | solution.py:23
  334.5 12.2 %collective-permute-start = (bf16[8,128,128]{2,0,1:T(8,128)(2,1)S(1)}, bf16[8,128,128]{2,0,1:T(8,128)(2,1)S(1)}, u32[]{:S(2)}, u32[]{:S(2)}) collective-permute-start(bf16[8,128,128]{2,0,1:T(8,128)(2,1)S(1)} %copy.47), channel_id=1, source_target_pairs={{1,0},{2,1},{3,2},{4,3},{5,4},{6,5},{7,6},{8,7},{9,8},{10,9},{11,1... | collective-permute-start | bytes 786440 | tf_op jit(solution)/shard_map/while/body/eval_jaxpr/ppermute | solution.py:23
  335.6 11.2 %collective-permute-start.2 = (bf16[8,128,128]{2,0,1:T(8,128)(2,1)S(1)}, bf16[8,128,128]{2,0,1:T(8,128)(2,1)S(1)}, u32[]{:S(2)}, u32[]{:S(2)}) collective-permute-start(bf16[8,128,128]{2,0,1:T(8,128)(2,1)S(1)} %copy.49), channel_id=1, source_target_pairs={{16,0},{32,16},{48,32},{64,48},{80,64},{96,80},{112,96},{128,112},... | collective-permute-start | bytes 786440 | tf_op jit(solution)/shard_map/while/body/eval_jaxpr/ppermute | solution.py:23
  337.3 9.5 %collective-permute-start.1 = (s32[8]{0:T(128)S(1)}, s32[8]{0:T(128)S(1)}, u32[]{:S(2)}, u32[]{:S(2)}) collective-permute-start(s32[8]{0:T(128)S(1)} %copy.48), channel_id=1, source_target_pairs={{1,0},{2,1},{3,2},{4,3},{5,4},{6,5},{7,6},{8,7},{9,8},{10,9},{11,1... | collective-permute-start | bytes 104 | tf_op jit(solution)/shard_map/while/body/eval_jaxpr/ppermute | solution.py:23
  346.8 12.2 %collective-permute-start = (bf16[8,128,128]{2,0,1:T(8,128)(2,1)S(1)}, bf16[8,128,128]{2,0,1:T(8,128)(2,1)S(1)}, u32[]{:S(2)}, u32[]{:S(2)}) collective-permute-start(bf16[8,128,128]{2,0,1:T(8,128)(2,1)S(1)} %copy.47), channel_id=1, source_target_pairs={{1,0},{2,1},{3,2},{4,3},{5,4},{6,5},{7,6},{8,7},{9,8},{10,9},{11,1... | collective-permute-start | bytes 786440 | tf_op jit(solution)/shard_map/while/body/eval_jaxpr/ppermute | solution.py:23
  347.8 11.2 %collective-permute-start.2 = (bf16[8,128,128]{2,0,1:T(8,128)(2,1)S(1)}, bf16[8,128,128]{2,0,1:T(8,128)(2,1)S(1)}, u32[]{:S(2)}, u32[]{:S(2)}) collective-permute-start(bf16[8,128,128]{2,0,1:T(8,128)(2,1)S(1)} %copy.49), channel_id=1, source_target_pairs={{16,0},{32,16},{48,32},{64,48},{80,64},{96,80},{112,96},{128,112},... | collective-permute-start | bytes 786440 | tf_op jit(solution)/shard_map/while/body/eval_jaxpr/ppermute | solution.py:23
  349.6 9.5 %collective-permute-start.1 = (s32[8]{0:T(128)S(1)}, s32[8]{0:T(128)S(1)}, u32[]{:S(2)}, u32[]{:S(2)}) collective-permute-start(s32[8]{0:T(128)S(1)} %copy.48), channel_id=1, source_target_pairs={{1,0},{2,1},{3,2},{4,3},{5,4},{6,5},{7,6},{8,7},{9,8},{10,9},{11,1... | collective-permute-start | bytes 104 | tf_op jit(solution)/shard_map/while/body/eval_jaxpr/ppermute | solution.py:23
  359.1 12.2 %collective-permute-start = (bf16[8,128,128]{2,0,1:T(8,128)(2,1)S(1)}, bf16[8,128,128]{2,0,1:T(8,128)(2,1)S(1)}, u32[]{:S(2)}, u32[]{:S(2)}) collective-permute-start(bf16[8,128,128]{2,0,1:T(8,128)(2,1)S(1)} %copy.47), channel_id=1, source_target_pairs={{1,0},{2,1},{3,2},{4,3},{5,4},{6,5},{7,6},{8,7},{9,8},{10,9},{11,1... | collective-permute-start | bytes 786440 | tf_op jit(solution)/shard_map/while/body/eval_jaxpr/ppermute | solution.py:23
  360.1 11.2 %collective-permute-start.2 = (bf16[8,128,128]{2,0,1:T(8,128)(2,1)S(1)}, bf16[8,128,128]{2,0,1:T(8,128)(2,1)S(1)}, u32[]{:S(2)}, u32[]{:S(2)}) collective-permute-start(bf16[8,128,128]{2,0,1:T(8,128)(2,1)S(1)} %copy.49), channel_id=1, source_target_pairs={{16,0},{32,16},{48,32},{64,48},{80,64},{96,80},{112,96},{128,112},... | collective-permute-start | bytes 786440 | tf_op jit(solution)/shard_map/while/body/eval_jaxpr/ppermute | solution.py:23
  361.8 9.5 %collective-permute-start.1 = (s32[8]{0:T(128)S(1)}, s32[8]{0:T(128)S(1)}, u32[]{:S(2)}, u32[]{:S(2)}) collective-permute-start(s32[8]{0:T(128)S(1)} %copy.48), channel_id=1, source_target_pairs={{1,0},{2,1},{3,2},{4,3},{5,4},{6,5},{7,6},{8,7},{9,8},{10,9},{11,1... | collective-permute-start | bytes 104 | tf_op jit(solution)/shard_map/while/body/eval_jaxpr/ppermute | solution.py:23
  (35 other events, 172.9 us)
Sparse Core Ops, SparseCore 0:
  11.3 117.2 all-reduce.1
where the time goes:
time: 389 us; the launch traced here: 387 us
  starting transfers between devices  119 us (31%)
  waiting for transfers between devices  110 us (28%)
  matrix products  70.5 us (18%)
  local copies, waits for them, and re-layouts  63.9 us (16%)
  between operations  16.2 us (4%)
  other arithmetic  5.74 us (1%)
    ppermute x76, starting transfers between devices, shifted(): return lax.ppermute(block, axis, route)  119 us
    psum x1, waiting for transfers between devices, from_root(): return lax.psum(block, axis)  91.7 us
    dot_general x16, matrix products, step_product(): jnp.einsum('qak,kqb->qab', left_rows, right_cols, preferred_element_type=...  44.2 us
    reshape x16, local copies, waits for them, and re-layouts, step_product(): left_rows.astype(jnp.bfloat16).reshape(q_row.shape[0], 128, tile_cols * 128)  36.8 us
    ppermute x76, waiting for transfers between devices, shifted(): return lax.ppermute(block, axis, route)  18.6 us
    while x90, local copies, waits for them, and re-layouts  14.1 us
    dot_general x16, matrix products, step_product(): jnp.einsum('pqk,pab->qakb', pick_left, p_blocks, preferred_element_type=j...  10.8 us
    dot_general x16, matrix products, step_product(): jnp.einsum('skq,sab->kaqb', pick_right, s_blocks, preferred_element_type=...  10.8 us
  transfers between devices with their start and end apart: 77, of which 7 were waited for; matrix products, arithmetic and copies ran while one was open for 29% of the time, Pallas kernels for 0%

commit v1 on v0

--- a/solution.py
+++ b/solution.py
@@ -6,7 +6,7 @@
 
 def from_root(block, axis, source):
     block = jnp.where(lax.axis_index(axis) == source, block, jnp.zeros_like(block))
-    return lax.psum(block, axis)
+    return jnp.sum(lax.all_gather(block, axis), axis=0)
 
 
 def shortened(shard):

time: 389 us -> 670 us (1.72)
  waiting for transfers between devices: 110 us -> 373 us
  other arithmetic: 5.74 us -> 29.5 us
  local copies, waits for them, and re-layouts: 63.9 us -> 49.5 us
  matrix products: 70.5 us -> 80.8 us
    all_gather x0 -> x1, waiting for transfers between devices: none -> 352 us  [from_root(): return jnp.sum(lax.all_gather(block, axis), axis=0)]
    psum x1 -> x0, waiting for transfers between devices: 91.7 us -> none  [from_root(): return lax.psum(block, axis)]
    reduce_sum x0 -> x1, other arithmetic: none -> 23.8 us  [from_root(): return jnp.sum(lax.all_gather(block, axis), axis=0)]
    while x90 -> x60, local copies, waits for them, and re-layouts: 14.1 us -> 0.6 us
    dot_general x16, matrix products: 44.2 us -> 54.5 us  [step_product(): jnp.einsum('qak,kqb->qab', left_rows, right_cols, preferred_element_type=...]
  transfers between devices with their start and end apart: 77 -> 77, of which waited for: 7 -> 7; matrix products, arithmetic and copies ran while one was open for 29% -> 22% of each run, Pallas kernels for 0% -> 0%
where the time goes in v1:
time: 670 us
  waiting for transfers between devices  373 us (56%)
  starting transfers between devices  119 us (18%)
  matrix products  80.8 us (12%)
  local copies, waits for them, and re-layouts  49.5 us (7%)
  other arithmetic  29.5 us (4%)
  between operations  16.2 us (2%)
    all_gather x1, waiting for transfers between devices, from_root(): return jnp.sum(lax.all_gather(block, axis), axis=0)  352 us
    ppermute x76, starting transfers between devices, shifted(): return lax.ppermute(block, axis, route)  119 us
    dot_general x16, matrix products, step_product(): jnp.einsum('qak,kqb->qab', left_rows, right_cols, preferred_element_type=...  54.5 us
    reshape x16, local copies, waits for them, and re-layouts, step_product(): left_rows.astype(jnp.bfloat16).reshape(q_row.shape[0], 128, tile_cols * 128)  36.9 us
    reduce_sum x1, other arithmetic, from_root(): return jnp.sum(lax.all_gather(block, axis), axis=0)  23.8 us
    ppermute x76, waiting for transfers between devices, shifted(): return lax.ppermute(block, axis, route)  20.5 us
  transfers between devices with their start and end apart: 77, of which 7 were waited for; matrix products, arithmetic and copies ran while one was open for 22% of the time, Pallas kernels for 0%

profile of v1, /device:TPU:1, one launch (start us, length us, event | category | flops | bytes accessed | tf_op | source)
XLA Modules:
  0.0 669.7 jit_solution(5324117171108534710)
XLA Ops:
  7.2 2.3 broadcast_select_fusion
  10.6 5.8 collective-permute-start.12
  20.4 5.0 gather_fusion
  25.7 8.2 %collective-permute-start.9 = (s32[8]{0:T(128)S(1)}, s32[8]{0:T(128)S(1)}, u32[]{:S(2)}, u32[]{:S(2)}) collective-permute-start(s32[8]{0:T(128)S(1)} %broadcast_select_fusion.13), channel_id=1, source_target_pairs={{2,0},{3,1},{4,2},{5,3},{6,4},{7,5},{8,6},{9,7},{10,8},{11,9},{12,... | collective-permute-start | bytes 104 | tf_op jit(solution)/shard_map/ppermute | solution.py:23
  36.4 352.1 %all-gather.3.cloned.1.call-done = bf16[16384,2048]{1,0:T(8,128)(2,1)} async-done(((bf16[1024,2048]{1,0:T(8,128)(2,1)}), bf16[16384,2048]{1,0:T(8,128)(2,1)}) %all-gather.3.cloned.1.call-update) | async-done | bytes 67108880 | tf_op jit(solution)/shard_map/all_gather | solution.py:9
  388.6 23.8 %reduce_sum.12 = bf16[1024,2048]{1,0:T(8,128)(2,1)} reduce(bf16[16,1024,2048]{2,1,0:T(8,128)(2,1)} %bitcast.4, bf16[]{:T(256)} %constant.338.clone.1), dimensions={0}, to_apply=%region_0.1 | reduce | flops 31457280 | bytes 71303168 | tf_op jit(solution)/shard_map/reduce_sum | solution.py:9
  412.3 5.0 gather_fusion.1
  417.3 4.7 fusion.18
  422.9 2.7 collective-permute-start.19
  428.1 4.1 collective-permute-start.5
  432.2 2.9 collective-permute-start.11
  435.1 3.0 collective-permute-start.14
  439.4 4.7 collective-permute-done.14
  447.5 3.4 collective-permute-start.7
  450.9 2.2 collective-permute-done.15
  453.1 11.1 %collective-permute-done.7 = bf16[8,128,128]{2,1,0:T(8,128)(2,1)S(1)} collective-permute-done((bf16[8,128,128]{2,1,0:T(8,128)(2,1)S(1)}, bf16[8,128,128]{2,1,0:T(8,128)(2,1)S(1)}, u32[]{:S(2)}, u32[]{:S(2)}) %collective-permute-start.7) | collective-permute-done | bytes 262176 | tf_op jit(solution)/shard_map/ppermute | solution.py:23
  464.4 190.0 %while.25 = (s32[]{:T(128)}, f32[8,128,128]{2,1,0:T(8,128)}, bf16[8,128,128]{2,0,1:T(8,128)(2,1)S(1)}, s32[8]{0:T(128)S(1)}, bf16[8,128,128]{2,0,1:T(8,128)(2,1)...) while((s32[]{:T(128)}, f32[8,128,128]{2,1,0:T(8,128)}, ...), condition=%wide.region_2.3_spmd.clone, body=%wide.region_1.2_spmd.clone.sunk | while | flops 304351008 | bytes 17303432 | solution.py:121
  465.8 6.1 collective-permute-start.2
  471.9 3.7 collective-permute-start.1
  478.1 2.3 reshape.449
  481.1 3.4 fusion.49
  489.1 2.3 reshape.449
  492.1 3.4 fusion.49
  495.9 2.9 collective-permute-start.2
  500.6 2.3 reshape.449
  503.6 3.4 fusion.49
  508.2 2.9 collective-permute-start.2
  512.9 2.3 reshape.449
  515.9 3.4 fusion.49
  520.5 2.9 collective-permute-start.2
  525.2 2.3 reshape.449
  528.2 3.4 fusion.49
  532.7 2.9 collective-permute-start.2
  537.5 2.3 reshape.449
  540.5 3.4 fusion.49
  545.0 2.9 collective-permute-start.2
  549.8 2.3 reshape.449
  552.8 3.4 fusion.49
  557.3 2.9 collective-permute-start.2
  562.0 2.3 reshape.449
  565.0 3.4 fusion.49
  569.6 2.9 collective-permute-start.2
  574.3 2.3 reshape.449
  577.3 3.4 fusion.49
  581.9 2.9 collective-permute-start.2
  586.6 2.3 reshape.449
  589.6 3.4 fusion.49
  594.1 2.9 collective-permute-start.2
  598.9 2.3 reshape.449
  601.9 3.4 fusion.49
  606.4 2.9 collective-permute-start.2
  611.1 2.3 reshape.449
  614.1 3.4 fusion.49
  618.7 2.9 collective-permute-start.2
  623.4 2.3 reshape.449
  626.4 3.4 fusion.49
  631.0 2.9 collective-permute-start.2
  635.7 2.3 reshape.449
  638.7 3.4 fusion.49
  643.2 2.9 collective-permute-start.2
  648.0 2.3 reshape.449
  651.0 3.4 fusion.49
  655.2 2.3 reshape.418
  659.1 2.8 fusion.15
  (361 shorter events, 71.9 us)
Async XLA Ops:
  7.2 381.4 %all-gather.3.cloned.1.call-start = ((), (), s32[]{:S(2)}) async-start(), calls=%async_computation | async-start | bytes 71303168 | tf_op jit(solution)/shard_map/all_gather | solution.py:9
  10.6 415.0 %collective-permute-start.12 = (bf16[8,128,128]{2,0,1:T(8,128)(2,1)S(1)}, bf16[8,128,128]{2,0,1:T(8,128)(2,1)S(1)}, u32[]{:S(2)}, u32[]{:S(2)}) collective-permute-start(bf16[8,128,128]{2,0,1:T(8,128)(2,1)S(1)} %bitcast.135), channel_id=1, source_target_pairs={{16,0},{32,16},{48,32},{64,48},{80,64},{96,80},{112,96},{128,112},... | collective-permute-start | bytes 786440 | tf_op jit(solution)/shard_map/ppermute | solution.py:23
  17.1 8.3 %collective-permute-start.16 = (s32[8]{0:T(128)S(1)}, s32[8]{0:T(128)S(1)}, u32[]{:S(2)}, u32[]{:S(2)}) collective-permute-start(s32[8]{0:T(128)S(1)} %compare_select_fusion.15), channel_id=1, source_target_pairs={{16,0},{32,16},{48,32},{64,48},{80,64},{96,80},{112,96},{128,112},... | collective-permute-start | bytes 104 | tf_op jit(solution)/shard_map/ppermute | solution.py:23
  18.4 7.3 %collective-permute-start.8 = (s32[8]{0:T(128)S(1)}, s32[8]{0:T(128)S(1)}, u32[]{:S(2)}, u32[]{:S(2)}) collective-permute-start(s32[8]{0:T(128)S(1)} %bitcast_select_fusion), channel_id=1, source_target_pairs={{1,0},{2,1},{3,2},{4,3},{5,4},{6,5},{7,6},{8,7},{9,8},{10,9},{11,1... | collective-permute-start | bytes 104 | tf_op jit(solution)/shard_map/ppermute | solution.py:23
  25.4 8.5 %collective-permute-start.17 = (s32[8]{0:T(128)S(1)}, s32[8]{0:T(128)S(1)}, u32[]{:S(2)}, u32[]{:S(2)}) collective-permute-start(s32[8]{0:T(128)S(1)} %broadcast_select_fusion.9), channel_id=1, source_target_pairs={{32,0},{48,16},{64,32},{80,48},{96,64},{112,80},{128,96},{144,112}... | collective-permute-start | bytes 104 | tf_op jit(solution)/shard_map/ppermute | solution.py:23
  25.7 8.9 %collective-permute-start.9 = (s32[8]{0:T(128)S(1)}, s32[8]{0:T(128)S(1)}, u32[]{:S(2)}, u32[]{:S(2)}) collective-permute-start(s32[8]{0:T(128)S(1)} %broadcast_select_fusion.13), channel_id=1, source_target_pairs={{2,0},{3,1},{4,2},{5,3},{6,4},{7,5},{8,6},{9,7},{10,8},{11,9},{12,... | collective-permute-start | bytes 104 | tf_op jit(solution)/shard_map/ppermute | solution.py:23
  33.9 388.9 %collective-permute-start.18 = (s32[8]{0:T(128)S(1)}, s32[8]{0:T(128)S(1)}, u32[]{:S(2)}, u32[]{:S(2)}) collective-permute-start(s32[8]{0:T(128)S(1)} %broadcast_select_fusion.10), channel_id=1, source_target_pairs={{64,0},{80,16},{96,32},{112,48},{128,64},{144,80},{160,96},{176,11... | collective-permute-start | bytes 104 | tf_op jit(solution)/shard_map/ppermute | solution.py:23
  34.7 397.5 %collective-permute-start.10 = (s32[8]{0:T(128)S(1)}, s32[8]{0:T(128)S(1)}, u32[]{:S(2)}, u32[]{:S(2)}) collective-permute-start(s32[8]{0:T(128)S(1)} %broadcast_select_fusion.14), channel_id=1, source_target_pairs={{4,0},{5,1},{6,2},{7,3},{8,4},{9,5},{10,6},{11,7},{12,8},{13,9},{1... | collective-permute-start | bytes 104 | tf_op jit(solution)/shard_map/ppermute | solution.py:23
  422.9 16.5 %collective-permute-start.19 = (s32[8]{0:T(128)S(1)}, s32[8]{0:T(128)S(1)}, u32[]{:S(2)}, u32[]{:S(2)}) collective-permute-start(s32[8]{0:T(128)S(1)} %broadcast_select_fusion.11), channel_id=1, source_target_pairs={{128,0},{144,16},{160,32},{176,48},{192,64},{208,80},{224,96},{240... | collective-permute-start | bytes 104 | tf_op jit(solution)/shard_map/ppermute | solution.py:23
  425.7 9.3 %collective-permute-start.13 = (bf16[8,128,128]{2,0,1:T(8,128)(2,1)S(1)}, bf16[8,128,128]{2,0,1:T(8,128)(2,1)S(1)}, u32[]{:S(2)}, u32[]{:S(2)}) collective-permute-start(bf16[8,128,128]{2,0,1:T(8,128)(2,1)S(1)} %broadcast_select_fusion.1), channel_id=1, source_target_pairs={{32,0},{48,16},{64,32},{80,48},{96,64},{112,80},{128,96},{144,112}... | collective-permute-start | bytes 786440 | tf_op jit(solution)/shard_map/ppermute | solution.py:23
  428.1 9.9 %collective-permute-start.5 = (bf16[8,128,128]{2,1,0:T(8,128)(2,1)S(1)}, bf16[8,128,128]{2,1,0:T(8,128)(2,1)S(1)}, u32[]{:S(2)}, u32[]{:S(2)}) collective-permute-start(bf16[8,128,128]{2,1,0:T(8,128)(2,1)S(1)} %broadcast_select_fusion.5), channel_id=1, source_target_pairs={{2,0},{3,1},{4,2},{5,3},{6,4},{7,5},{8,6},{9,7},{10,8},{11,9},{12,... | collective-permute-start | bytes 786440 | tf_op jit(solution)/shard_map/ppermute | solution.py:23
  432.2 18.7 %collective-permute-start.11 = (s32[8]{0:T(128)S(1)}, s32[8]{0:T(128)S(1)}, u32[]{:S(2)}, u32[]{:S(2)}) collective-permute-start(s32[8]{0:T(128)S(1)} %broadcast_select_fusion.15), channel_id=1, source_target_pairs={{8,0},{9,1},{10,2},{11,3},{12,4},{13,5},{14,6},{15,7},{0,8},{1,9},... | collective-permute-start | bytes 104 | tf_op jit(solution)/shard_map/ppermute | solution.py:23
  435.1 9.0 %collective-permute-start.14 = (bf16[8,128,128]{2,0,1:T(8,128)(2,1)S(1)}, bf16[8,128,128]{2,0,1:T(8,128)(2,1)S(1)}, u32[]{:S(2)}, u32[]{:S(2)}) collective-permute-start(bf16[8,128,128]{2,0,1:T(8,128)(2,1)S(1)} %broadcast_select_fusion.2), channel_id=1, source_target_pairs={{64,0},{80,16},{96,32},{112,48},{128,64},{144,80},{160,96},{176,11... | collective-permute-start | bytes 786440 | tf_op jit(solution)/shard_map/ppermute | solution.py:23
  438.1 9.3 %collective-permute-start.6 = (bf16[8,128,128]{2,1,0:T(8,128)(2,1)S(1)}, bf16[8,128,128]{2,1,0:T(8,128)(2,1)S(1)}, u32[]{:S(2)}, u32[]{:S(2)}) collective-permute-start(bf16[8,128,128]{2,1,0:T(8,128)(2,1)S(1)} %broadcast_select_fusion.6), channel_id=1, source_target_pairs={{4,0},{5,1},{6,2},{7,3},{8,4},{9,5},{10,6},{11,7},{12,8},{13,9},{1... | collective-permute-start | bytes 786440 | tf_op jit(solution)/shard_map/ppermute | solution.py:23
  444.1 9.0 %collective-permute-start.15 = (bf16[8,128,128]{2,0,1:T(8,128)(2,1)S(1)}, bf16[8,128,128]{2,0,1:T(8,128)(2,1)S(1)}, u32[]{:S(2)}, u32[]{:S(2)}) collective-permute-start(bf16[8,128,128]{2,0,1:T(8,128)(2,1)S(1)} %broadcast_select_fusion.3), channel_id=1, source_target_pairs={{128,0},{144,16},{160,32},{176,48},{192,64},{208,80},{224,96},{240... | collective-permute-start | bytes 786440 | tf_op jit(solution)/shard_map/ppermute | solution.py:23
  447.5 16.7 %collective-permute-start.7 = (bf16[8,128,128]{2,1,0:T(8,128)(2,1)S(1)}, bf16[8,128,128]{2,1,0:T(8,128)(2,1)S(1)}, u32[]{:S(2)}, u32[]{:S(2)}) collective-permute-start(bf16[8,128,128]{2,1,0:T(8,128)(2,1)S(1)} %broadcast_select_fusion.7), channel_id=1, source_target_pairs={{8,0},{9,1},{10,2},{11,3},{12,4},{13,5},{14,6},{15,7},{0,8},{1,9},... | collective-permute-start | bytes 786440 | tf_op jit(solution)/shard_map/ppermute | solution.py:23
  464.5 20.0 %collective-permute-start = (bf16[8,128,128]{2,0,1:T(8,128)(2,1)S(1)}, bf16[8,128,128]{2,0,1:T(8,128)(2,1)S(1)}, u32[]{:S(2)}, u32[]{:S(2)}) collective-permute-start(bf16[8,128,128]{2,0,1:T(8,128)(2,1)S(1)} %copy.46), channel_id=1, source_target_pairs={{1,0},{2,1},{3,2},{4,3},{5,4},{6,5},{7,6},{8,7},{9,8},{10,9},{11,1... | collective-permute-start | bytes 786440 | tf_op jit(solution)/shard_map/while/body/eval_jaxpr/ppermute | solution.py:23
  465.8 18.7 %collective-permute-start.2 = (bf16[8,128,128]{2,0,1:T(8,128)(2,1)S(1)}, bf16[8,128,128]{2,0,1:T(8,128)(2,1)S(1)}, u32[]{:S(2)}, u32[]{:S(2)}) collective-permute-start(bf16[8,128,128]{2,0,1:T(8,128)(2,1)S(1)} %copy.48), channel_id=1, source_target_pairs={{16,0},{32,16},{48,32},{64,48},{80,64},{96,80},{112,96},{128,112},... | collective-permute-start | bytes 786440 | tf_op jit(solution)/shard_map/while/body/eval_jaxpr/ppermute | solution.py:23
  471.9 12.6 %collective-permute-start.1 = (s32[8]{0:T(128)S(1)}, s32[8]{0:T(128)S(1)}, u32[]{:S(2)}, u32[]{:S(2)}) collective-permute-start(s32[8]{0:T(128)S(1)} %copy.47), channel_id=1, source_target_pairs={{1,0},{2,1},{3,2},{4,3},{5,4},{6,5},{7,6},{8,7},{9,8},{10,9},{11,1... | collective-permute-start | bytes 104 | tf_op jit(solution)/shard_map/while/body/eval_jaxpr/ppermute | solution.py:23
  475.5 8.9 %collective-permute-start.3 = (s32[8]{0:T(128)S(1)}, s32[8]{0:T(128)S(1)}, u32[]{:S(2)}, u32[]{:S(2)}) collective-permute-start(s32[8]{0:T(128)S(1)} %copy.49), channel_id=1, source_target_pairs={{16,0},{32,16},{48,32},{64,48},{80,64},{96,80},{112,96},{128,112},... | collective-permute-start | bytes 104 | tf_op jit(solution)/shard_map/while/body/eval_jaxpr/ppermute | solution.py:23
  484.5 11.0 %collective-permute-start = (bf16[8,128,128]{2,0,1:T(8,128)(2,1)S(1)}, bf16[8,128,128]{2,0,1:T(8,128)(2,1)S(1)}, u32[]{:S(2)}, u32[]{:S(2)}) collective-permute-start(bf16[8,128,128]{2,0,1:T(8,128)(2,1)S(1)} %copy.46), channel_id=1, source_target_pairs={{1,0},{2,1},{3,2},{4,3},{5,4},{6,5},{7,6},{8,7},{9,8},{10,9},{11,1... | collective-permute-start | bytes 786440 | tf_op jit(solution)/shard_map/while/body/eval_jaxpr/ppermute | solution.py:23
  485.1 10.4 %collective-permute-start.2 = (bf16[8,128,128]{2,0,1:T(8,128)(2,1)S(1)}, bf16[8,128,128]{2,0,1:T(8,128)(2,1)S(1)}, u32[]{:S(2)}, u32[]{:S(2)}) collective-permute-start(bf16[8,128,128]{2,0,1:T(8,128)(2,1)S(1)} %copy.48), channel_id=1, source_target_pairs={{16,0},{32,16},{48,32},{64,48},{80,64},{96,80},{112,96},{128,112},... | collective-permute-start | bytes 786440 | tf_op jit(solution)/shard_map/while/body/eval_jaxpr/ppermute | solution.py:23
  486.6 9.0 %collective-permute-start.1 = (s32[8]{0:T(128)S(1)}, s32[8]{0:T(128)S(1)}, u32[]{:S(2)}, u32[]{:S(2)}) collective-permute-start(s32[8]{0:T(128)S(1)} %copy.47), channel_id=1, source_target_pairs={{1,0},{2,1},{3,2},{4,3},{5,4},{6,5},{7,6},{8,7},{9,8},{10,9},{11,1... | collective-permute-start | bytes 104 | tf_op jit(solution)/shard_map/while/body/eval_jaxpr/ppermute | solution.py:23
  487.5 8.0 %collective-permute-start.3 = (s32[8]{0:T(128)S(1)}, s32[8]{0:T(128)S(1)}, u32[]{:S(2)}, u32[]{:S(2)}) collective-permute-start(s32[8]{0:T(128)S(1)} %copy.49), channel_id=1, source_target_pairs={{16,0},{32,16},{48,32},{64,48},{80,64},{96,80},{112,96},{128,112},... | collective-permute-start | bytes 104 | tf_op jit(solution)/shard_map/while/body/eval_jaxpr/ppermute | solution.py:23
  495.6 11.5 %collective-permute-start = (bf16[8,128,128]{2,0,1:T(8,128)(2,1)S(1)}, bf16[8,128,128]{2,0,1:T(8,128)(2,1)S(1)}, u32[]{:S(2)}, u32[]{:S(2)}) collective-permute-start(bf16[8,128,128]{2,0,1:T(8,128)(2,1)S(1)} %copy.46), channel_id=1, source_target_pairs={{1,0},{2,1},{3,2},{4,3},{5,4},{6,5},{7,6},{8,7},{9,8},{10,9},{11,1... | collective-permute-start | bytes 786440 | tf_op jit(solution)/shard_map/while/body/eval_jaxpr/ppermute | solution.py:23
  495.9 11.2 %collective-permute-start.2 = (bf16[8,128,128]{2,0,1:T(8,128)(2,1)S(1)}, bf16[8,128,128]{2,0,1:T(8,128)(2,1)S(1)}, u32[]{:S(2)}, u32[]{:S(2)}) collective-permute-start(bf16[8,128,128]{2,0,1:T(8,128)(2,1)S(1)} %copy.48), channel_id=1, source_target_pairs={{16,0},{32,16},{48,32},{64,48},{80,64},{96,80},{112,96},{128,112},... | collective-permute-start | bytes 786440 | tf_op jit(solution)/shard_map/while/body/eval_jaxpr/ppermute | solution.py:23
  498.8 8.3 %collective-permute-start.1 = (s32[8]{0:T(128)S(1)}, s32[8]{0:T(128)S(1)}, u32[]{:S(2)}, u32[]{:S(2)}) collective-permute-start(s32[8]{0:T(128)S(1)} %copy.47), channel_id=1, source_target_pairs={{1,0},{2,1},{3,2},{4,3},{5,4},{6,5},{7,6},{8,7},{9,8},{10,9},{11,1... | collective-permute-start | bytes 104 | tf_op jit(solution)/shard_map/while/body/eval_jaxpr/ppermute | solution.py:23
  507.2 12.2 %collective-permute-start = (bf16[8,128,128]{2,0,1:T(8,128)(2,1)S(1)}, bf16[8,128,128]{2,0,1:T(8,128)(2,1)S(1)}, u32[]{:S(2)}, u32[]{:S(2)}) collective-permute-start(bf16[8,128,128]{2,0,1:T(8,128)(2,1)S(1)} %copy.46), channel_id=1, source_target_pairs={{1,0},{2,1},{3,2},{4,3},{5,4},{6,5},{7,6},{8,7},{9,8},{10,9},{11,1... | collective-permute-start | bytes 786440 | tf_op jit(solution)/shard_map/while/body/eval_jaxpr/ppermute | solution.py:23
  508.2 11.2 %collective-permute-start.2 = (bf16[8,128,128]{2,0,1:T(8,128)(2,1)S(1)}, bf16[8,128,128]{2,0,1:T(8,128)(2,1)S(1)}, u32[]{:S(2)}, u32[]{:S(2)}) collective-permute-start(bf16[8,128,128]{2,0,1:T(8,128)(2,1)S(1)} %copy.48), channel_id=1, source_target_pairs={{16,0},{32,16},{48,32},{64,48},{80,64},{96,80},{112,96},{128,112},... | collective-permute-start | bytes 786440 | tf_op jit(solution)/shard_map/while/body/eval_jaxpr/ppermute | solution.py:23
  511.1 8.3 %collective-permute-start.1 = (s32[8]{0:T(128)S(1)}, s32[8]{0:T(128)S(1)}, u32[]{:S(2)}, u32[]{:S(2)}) collective-permute-start(s32[8]{0:T(128)S(1)} %copy.47), channel_id=1, source_target_pairs={{1,0},{2,1},{3,2},{4,3},{5,4},{6,5},{7,6},{8,7},{9,8},{10,9},{11,1... | collective-permute-start | bytes 104 | tf_op jit(solution)/shard_map/while/body/eval_jaxpr/ppermute | solution.py:23
  519.4 12.2 %collective-permute-start = (bf16[8,128,128]{2,0,1:T(8,128)(2,1)S(1)}, bf16[8,128,128]{2,0,1:T(8,128)(2,1)S(1)}, u32[]{:S(2)}, u32[]{:S(2)}) collective-permute-start(bf16[8,128,128]{2,0,1:T(8,128)(2,1)S(1)} %copy.46), channel_id=1, source_target_pairs={{1,0},{2,1},{3,2},{4,3},{5,4},{6,5},{7,6},{8,7},{9,8},{10,9},{11,1... | collective-permute-start | bytes 786440 | tf_op jit(solution)/shard_map/while/body/eval_jaxpr/ppermute | solution.py:23
  520.5 11.2 %collective-permute-start.2 = (bf16[8,128,128]{2,0,1:T(8,128)(2,1)S(1)}, bf16[8,128,128]{2,0,1:T(8,128)(2,1)S(1)}, u32[]{:S(2)}, u32[]{:S(2)}) collective-permute-start(bf16[8,128,128]{2,0,1:T(8,128)(2,1)S(1)} %copy.48), channel_id=1, source_target_pairs={{16,0},{32,16},{48,32},{64,48},{80,64},{96,80},{112,96},{128,112},... | collective-permute-start | bytes 786440 | tf_op jit(solution)/shard_map/while/body/eval_jaxpr/ppermute | solution.py:23
  523.4 8.3 %collective-permute-start.1 = (s32[8]{0:T(128)S(1)}, s32[8]{0:T(128)S(1)}, u32[]{:S(2)}, u32[]{:S(2)}) collective-permute-start(s32[8]{0:T(128)S(1)} %copy.47), channel_id=1, source_target_pairs={{1,0},{2,1},{3,2},{4,3},{5,4},{6,5},{7,6},{8,7},{9,8},{10,9},{11,1... | collective-permute-start | bytes 104 | tf_op jit(solution)/shard_map/while/body/eval_jaxpr/ppermute | solution.py:23
  531.7 12.2 %collective-permute-start = (bf16[8,128,128]{2,0,1:T(8,128)(2,1)S(1)}, bf16[8,128,128]{2,0,1:T(8,128)(2,1)S(1)}, u32[]{:S(2)}, u32[]{:S(2)}) collective-permute-start(bf16[8,128,128]{2,0,1:T(8,128)(2,1)S(1)} %copy.46), channel_id=1, source_target_pairs={{1,0},{2,1},{3,2},{4,3},{5,4},{6,5},{7,6},{8,7},{9,8},{10,9},{11,1... | collective-permute-start | bytes 786440 | tf_op jit(solution)/shard_map/while/body/eval_jaxpr/ppermute | solution.py:23
  532.7 11.2 %collective-permute-start.2 = (bf16[8,128,128]{2,0,1:T(8,128)(2,1)S(1)}, bf16[8,128,128]{2,0,1:T(8,128)(2,1)S(1)}, u32[]{:S(2)}, u32[]{:S(2)}) collective-permute-start(bf16[8,128,128]{2,0,1:T(8,128)(2,1)S(1)} %copy.48), channel_id=1, source_target_pairs={{16,0},{32,16},{48,32},{64,48},{80,64},{96,80},{112,96},{128,112},... | collective-permute-start | bytes 786440 | tf_op jit(solution)/shard_map/while/body/eval_jaxpr/ppermute | solution.py:23
  535.7 8.3 %collective-permute-start.1 = (s32[8]{0:T(128)S(1)}, s32[8]{0:T(128)S(1)}, u32[]{:S(2)}, u32[]{:S(2)}) collective-permute-start(s32[8]{0:T(128)S(1)} %copy.47), channel_id=1, source_target_pairs={{1,0},{2,1},{3,2},{4,3},{5,4},{6,5},{7,6},{8,7},{9,8},{10,9},{11,1... | collective-permute-start | bytes 104 | tf_op jit(solution)/shard_map/while/body/eval_jaxpr/ppermute | solution.py:23
  544.0 12.2 %collective-permute-start = (bf16[8,128,128]{2,0,1:T(8,128)(2,1)S(1)}, bf16[8,128,128]{2,0,1:T(8,128)(2,1)S(1)}, u32[]{:S(2)}, u32[]{:S(2)}) collective-permute-start(bf16[8,128,128]{2,0,1:T(8,128)(2,1)S(1)} %copy.46), channel_id=1, source_target_pairs={{1,0},{2,1},{3,2},{4,3},{5,4},{6,5},{7,6},{8,7},{9,8},{10,9},{11,1... | collective-permute-start | bytes 786440 | tf_op jit(solution)/shard_map/while/body/eval_jaxpr/ppermute | solution.py:23
  545.0 11.2 %collective-permute-start.2 = (bf16[8,128,128]{2,0,1:T(8,128)(2,1)S(1)}, bf16[8,128,128]{2,0,1:T(8,128)(2,1)S(1)}, u32[]{:S(2)}, u32[]{:S(2)}) collective-permute-start(bf16[8,128,128]{2,0,1:T(8,128)(2,1)S(1)} %copy.48), channel_id=1, source_target_pairs={{16,0},{32,16},{48,32},{64,48},{80,64},{96,80},{112,96},{128,112},... | collective-permute-start | bytes 786440 | tf_op jit(solution)/shard_map/while/body/eval_jaxpr/ppermute | solution.py:23
  547.9 8.3 %collective-permute-start.1 = (s32[8]{0:T(128)S(1)}, s32[8]{0:T(128)S(1)}, u32[]{:S(2)}, u32[]{:S(2)}) collective-permute-start(s32[8]{0:T(128)S(1)} %copy.47), channel_id=1, source_target_pairs={{1,0},{2,1},{3,2},{4,3},{5,4},{6,5},{7,6},{8,7},{9,8},{10,9},{11,1... | collective-permute-start | bytes 104 | tf_op jit(solution)/shard_map/while/body/eval_jaxpr/ppermute | solution.py:23
  556.3 12.2 %collective-permute-start = (bf16[8,128,128]{2,0,1:T(8,128)(2,1)S(1)}, bf16[8,128,128]{2,0,1:T(8,128)(2,1)S(1)}, u32[]{:S(2)}, u32[]{:S(2)}) collective-permute-start(bf16[8,128,128]{2,0,1:T(8,128)(2,1)S(1)} %copy.46), channel_id=1, source_target_pairs={{1,0},{2,1},{3,2},{4,3},{5,4},{6,5},{7,6},{8,7},{9,8},{10,9},{11,1... | collective-permute-start | bytes 786440 | tf_op jit(solution)/shard_map/while/body/eval_jaxpr/ppermute | solution.py:23
  557.3 11.2 %collective-permute-start.2 = (bf16[8,128,128]{2,0,1:T(8,128)(2,1)S(1)}, bf16[8,128,128]{2,0,1:T(8,128)(2,1)S(1)}, u32[]{:S(2)}, u32[]{:S(2)}) collective-permute-start(bf16[8,128,128]{2,0,1:T(8,128)(2,1)S(1)} %copy.48), channel_id=1, source_target_pairs={{16,0},{32,16},{48,32},{64,48},{80,64},{96,80},{112,96},{128,112},... | collective-permute-start | bytes 786440 | tf_op jit(solution)/shard_map/while/body/eval_jaxpr/ppermute | solution.py:23
  560.2 8.3 %collective-permute-start.1 = (s32[8]{0:T(128)S(1)}, s32[8]{0:T(128)S(1)}, u32[]{:S(2)}, u32[]{:S(2)}) collective-permute-start(s32[8]{0:T(128)S(1)} %copy.47), channel_id=1, source_target_pairs={{1,0},{2,1},{3,2},{4,3},{5,4},{6,5},{7,6},{8,7},{9,8},{10,9},{11,1... | collective-permute-start | bytes 104 | tf_op jit(solution)/shard_map/while/body/eval_jaxpr/ppermute | solution.py:23
  568.5 12.2 %collective-permute-start = (bf16[8,128,128]{2,0,1:T(8,128)(2,1)S(1)}, bf16[8,128,128]{2,0,1:T(8,128)(2,1)S(1)}, u32[]{:S(2)}, u32[]{:S(2)}) collective-permute-start(bf16[8,128,128]{2,0,1:T(8,128)(2,1)S(1)} %copy.46), channel_id=1, source_target_pairs={{1,0},{2,1},{3,2},{4,3},{5,4},{6,5},{7,6},{8,7},{9,8},{10,9},{11,1... | collective-permute-start | bytes 786440 | tf_op jit(solution)/shard_map/while/body/eval_jaxpr/ppermute | solution.py:23
  569.6 11.2 %collective-permute-start.2 = (bf16[8,128,128]{2,0,1:T(8,128)(2,1)S(1)}, bf16[8,128,128]{2,0,1:T(8,128)(2,1)S(1)}, u32[]{:S(2)}, u32[]{:S(2)}) collective-permute-start(bf16[8,128,128]{2,0,1:T(8,128)(2,1)S(1)} %copy.48), channel_id=1, source_target_pairs={{16,0},{32,16},{48,32},{64,48},{80,64},{96,80},{112,96},{128,112},... | collective-permute-start | bytes 786440 | tf_op jit(solution)/shard_map/while/body/eval_jaxpr/ppermute | solution.py:23
  572.5 8.3 %collective-permute-start.1 = (s32[8]{0:T(128)S(1)}, s32[8]{0:T(128)S(1)}, u32[]{:S(2)}, u32[]{:S(2)}) collective-permute-start(s32[8]{0:T(128)S(1)} %copy.47), channel_id=1, source_target_pairs={{1,0},{2,1},{3,2},{4,3},{5,4},{6,5},{7,6},{8,7},{9,8},{10,9},{11,1... | collective-permute-start | bytes 104 | tf_op jit(solution)/shard_map/while/body/eval_jaxpr/ppermute | solution.py:23
  580.8 12.2 %collective-permute-start = (bf16[8,128,128]{2,0,1:T(8,128)(2,1)S(1)}, bf16[8,128,128]{2,0,1:T(8,128)(2,1)S(1)}, u32[]{:S(2)}, u32[]{:S(2)}) collective-permute-start(bf16[8,128,128]{2,0,1:T(8,128)(2,1)S(1)} %copy.46), channel_id=1, source_target_pairs={{1,0},{2,1},{3,2},{4,3},{5,4},{6,5},{7,6},{8,7},{9,8},{10,9},{11,1... | collective-permute-start | bytes 786440 | tf_op jit(solution)/shard_map/while/body/eval_jaxpr/ppermute | solution.py:23
  581.9 11.2 %collective-permute-start.2 = (bf16[8,128,128]{2,0,1:T(8,128)(2,1)S(1)}, bf16[8,128,128]{2,0,1:T(8,128)(2,1)S(1)}, u32[]{:S(2)}, u32[]{:S(2)}) collective-permute-start(bf16[8,128,128]{2,0,1:T(8,128)(2,1)S(1)} %copy.48), channel_id=1, source_target_pairs={{16,0},{32,16},{48,32},{64,48},{80,64},{96,80},{112,96},{128,112},... | collective-permute-start | bytes 786440 | tf_op jit(solution)/shard_map/while/body/eval_jaxpr/ppermute | solution.py:23
  584.8 8.3 %collective-permute-start.1 = (s32[8]{0:T(128)S(1)}, s32[8]{0:T(128)S(1)}, u32[]{:S(2)}, u32[]{:S(2)}) collective-permute-start(s32[8]{0:T(128)S(1)} %copy.47), channel_id=1, source_target_pairs={{1,0},{2,1},{3,2},{4,3},{5,4},{6,5},{7,6},{8,7},{9,8},{10,9},{11,1... | collective-permute-start | bytes 104 | tf_op jit(solution)/shard_map/while/body/eval_jaxpr/ppermute | solution.py:23
  593.1 12.2 %collective-permute-start = (bf16[8,128,128]{2,0,1:T(8,128)(2,1)S(1)}, bf16[8,128,128]{2,0,1:T(8,128)(2,1)S(1)}, u32[]{:S(2)}, u32[]{:S(2)}) collective-permute-start(bf16[8,128,128]{2,0,1:T(8,128)(2,1)S(1)} %copy.46), channel_id=1, source_target_pairs={{1,0},{2,1},{3,2},{4,3},{5,4},{6,5},{7,6},{8,7},{9,8},{10,9},{11,1... | collective-permute-start | bytes 786440 | tf_op jit(solution)/shard_map/while/body/eval_jaxpr/ppermute | solution.py:23
  594.1 11.2 %collective-permute-start.2 = (bf16[8,128,128]{2,0,1:T(8,128)(2,1)S(1)}, bf16[8,128,128]{2,0,1:T(8,128)(2,1)S(1)}, u32[]{:S(2)}, u32[]{:S(2)}) collective-permute-start(bf16[8,128,128]{2,0,1:T(8,128)(2,1)S(1)} %copy.48), channel_id=1, source_target_pairs={{16,0},{32,16},{48,32},{64,48},{80,64},{96,80},{112,96},{128,112},... | collective-permute-start | bytes 786440 | tf_op jit(solution)/shard_map/while/body/eval_jaxpr/ppermute | solution.py:23
  597.1 8.3 %collective-permute-start.1 = (s32[8]{0:T(128)S(1)}, s32[8]{0:T(128)S(1)}, u32[]{:S(2)}, u32[]{:S(2)}) collective-permute-start(s32[8]{0:T(128)S(1)} %copy.47), channel_id=1, source_target_pairs={{1,0},{2,1},{3,2},{4,3},{5,4},{6,5},{7,6},{8,7},{9,8},{10,9},{11,1... | collective-permute-start | bytes 104 | tf_op jit(solution)/shard_map/while/body/eval_jaxpr/ppermute | solution.py:23
  605.4 12.2 %collective-permute-start = (bf16[8,128,128]{2,0,1:T(8,128)(2,1)S(1)}, bf16[8,128,128]{2,0,1:T(8,128)(2,1)S(1)}, u32[]{:S(2)}, u32[]{:S(2)}) collective-permute-start(bf16[8,128,128]{2,0,1:T(8,128)(2,1)S(1)} %copy.46), channel_id=1, source_target_pairs={{1,0},{2,1},{3,2},{4,3},{5,4},{6,5},{7,6},{8,7},{9,8},{10,9},{11,1... | collective-permute-start | bytes 786440 | tf_op jit(solution)/shard_map/while/body/eval_jaxpr/ppermute | solution.py:23
  606.4 11.2 %collective-permute-start.2 = (bf16[8,128,128]{2,0,1:T(8,128)(2,1)S(1)}, bf16[8,128,128]{2,0,1:T(8,128)(2,1)S(1)}, u32[]{:S(2)}, u32[]{:S(2)}) collective-permute-start(bf16[8,128,128]{2,0,1:T(8,128)(2,1)S(1)} %copy.48), channel_id=1, source_target_pairs={{16,0},{32,16},{48,32},{64,48},{80,64},{96,80},{112,96},{128,112},... | collective-permute-start | bytes 786440 | tf_op jit(solution)/shard_map/while/body/eval_jaxpr/ppermute | solution.py:23
  609.3 8.3 %collective-permute-start.1 = (s32[8]{0:T(128)S(1)}, s32[8]{0:T(128)S(1)}, u32[]{:S(2)}, u32[]{:S(2)}) collective-permute-start(s32[8]{0:T(128)S(1)} %copy.47), channel_id=1, source_target_pairs={{1,0},{2,1},{3,2},{4,3},{5,4},{6,5},{7,6},{8,7},{9,8},{10,9},{11,1... | collective-permute-start | bytes 104 | tf_op jit(solution)/shard_map/while/body/eval_jaxpr/ppermute | solution.py:23
  617.7 12.2 %collective-permute-start = (bf16[8,128,128]{2,0,1:T(8,128)(2,1)S(1)}, bf16[8,128,128]{2,0,1:T(8,128)(2,1)S(1)}, u32[]{:S(2)}, u32[]{:S(2)}) collective-permute-start(bf16[8,128,128]{2,0,1:T(8,128)(2,1)S(1)} %copy.46), channel_id=1, source_target_pairs={{1,0},{2,1},{3,2},{4,3},{5,4},{6,5},{7,6},{8,7},{9,8},{10,9},{11,1... | collective-permute-start | bytes 786440 | tf_op jit(solution)/shard_map/while/body/eval_jaxpr/ppermute | solution.py:23
  618.7 11.2 %collective-permute-start.2 = (bf16[8,128,128]{2,0,1:T(8,128)(2,1)S(1)}, bf16[8,128,128]{2,0,1:T(8,128)(2,1)S(1)}, u32[]{:S(2)}, u32[]{:S(2)}) collective-permute-start(bf16[8,128,128]{2,0,1:T(8,128)(2,1)S(1)} %copy.48), channel_id=1, source_target_pairs={{16,0},{32,16},{48,32},{64,48},{80,64},{96,80},{112,96},{128,112},... | collective-permute-start | bytes 786440 | tf_op jit(solution)/shard_map/while/body/eval_jaxpr/ppermute | solution.py:23
  621.6 8.3 %collective-permute-start.1 = (s32[8]{0:T(128)S(1)}, s32[8]{0:T(128)S(1)}, u32[]{:S(2)}, u32[]{:S(2)}) collective-permute-start(s32[8]{0:T(128)S(1)} %copy.47), channel_id=1, source_target_pairs={{1,0},{2,1},{3,2},{4,3},{5,4},{6,5},{7,6},{8,7},{9,8},{10,9},{11,1... | collective-permute-start | bytes 104 | tf_op jit(solution)/shard_map/while/body/eval_jaxpr/ppermute | solution.py:23
  629.9 12.2 %collective-permute-start = (bf16[8,128,128]{2,0,1:T(8,128)(2,1)S(1)}, bf16[8,128,128]{2,0,1:T(8,128)(2,1)S(1)}, u32[]{:S(2)}, u32[]{:S(2)}) collective-permute-start(bf16[8,128,128]{2,0,1:T(8,128)(2,1)S(1)} %copy.46), channel_id=1, source_target_pairs={{1,0},{2,1},{3,2},{4,3},{5,4},{6,5},{7,6},{8,7},{9,8},{10,9},{11,1... | collective-permute-start | bytes 786440 | tf_op jit(solution)/shard_map/while/body/eval_jaxpr/ppermute | solution.py:23
  631.0 11.2 %collective-permute-start.2 = (bf16[8,128,128]{2,0,1:T(8,128)(2,1)S(1)}, bf16[8,128,128]{2,0,1:T(8,128)(2,1)S(1)}, u32[]{:S(2)}, u32[]{:S(2)}) collective-permute-start(bf16[8,128,128]{2,0,1:T(8,128)(2,1)S(1)} %copy.48), channel_id=1, source_target_pairs={{16,0},{32,16},{48,32},{64,48},{80,64},{96,80},{112,96},{128,112},... | collective-permute-start | bytes 786440 | tf_op jit(solution)/shard_map/while/body/eval_jaxpr/ppermute | solution.py:23
  633.9 8.3 %collective-permute-start.1 = (s32[8]{0:T(128)S(1)}, s32[8]{0:T(128)S(1)}, u32[]{:S(2)}, u32[]{:S(2)}) collective-permute-start(s32[8]{0:T(128)S(1)} %copy.47), channel_id=1, source_target_pairs={{1,0},{2,1},{3,2},{4,3},{5,4},{6,5},{7,6},{8,7},{9,8},{10,9},{11,1... | collective-permute-start | bytes 104 | tf_op jit(solution)/shard_map/while/body/eval_jaxpr/ppermute | solution.py:23
  634.9 7.3 %collective-permute-start.3 = (s32[8]{0:T(128)S(1)}, s32[8]{0:T(128)S(1)}, u32[]{:S(2)}, u32[]{:S(2)}) collective-permute-start(s32[8]{0:T(128)S(1)} %copy.49), channel_id=1, source_target_pairs={{16,0},{32,16},{48,32},{64,48},{80,64},{96,80},{112,96},{128,112},... | collective-permute-start | bytes 104 | tf_op jit(solution)/shard_map/while/body/eval_jaxpr/ppermute | solution.py:23
  642.2 12.2 %collective-permute-start = (bf16[8,128,128]{2,0,1:T(8,128)(2,1)S(1)}, bf16[8,128,128]{2,0,1:T(8,128)(2,1)S(1)}, u32[]{:S(2)}, u32[]{:S(2)}) collective-permute-start(bf16[8,128,128]{2,0,1:T(8,128)(2,1)S(1)} %copy.46), channel_id=1, source_target_pairs={{1,0},{2,1},{3,2},{4,3},{5,4},{6,5},{7,6},{8,7},{9,8},{10,9},{11,1... | collective-permute-start | bytes 786440 | tf_op jit(solution)/shard_map/while/body/eval_jaxpr/ppermute | solution.py:23
  643.2 11.2 %collective-permute-start.2 = (bf16[8,128,128]{2,0,1:T(8,128)(2,1)S(1)}, bf16[8,128,128]{2,0,1:T(8,128)(2,1)S(1)}, u32[]{:S(2)}, u32[]{:S(2)}) collective-permute-start(bf16[8,128,128]{2,0,1:T(8,128)(2,1)S(1)} %copy.48), channel_id=1, source_target_pairs={{16,0},{32,16},{48,32},{64,48},{80,64},{96,80},{112,96},{128,112},... | collective-permute-start | bytes 786440 | tf_op jit(solution)/shard_map/while/body/eval_jaxpr/ppermute | solution.py:23
  646.2 8.2 %collective-permute-start.1 = (s32[8]{0:T(128)S(1)}, s32[8]{0:T(128)S(1)}, u32[]{:S(2)}, u32[]{:S(2)}) collective-permute-start(s32[8]{0:T(128)S(1)} %copy.47), channel_id=1, source_target_pairs={{1,0},{2,1},{3,2},{4,3},{5,4},{6,5},{7,6},{8,7},{9,8},{10,9},{11,1... | collective-permute-start | bytes 104 | tf_op jit(solution)/shard_map/while/body/eval_jaxpr/ppermute | solution.py:23
  (20 other events, 163.0 us)
Sparse Core Ops, SparseCore 0:
  10.4 378.1 all-gather.2
